TPU v7x, 128 devices: a whole 4x4x4 slice. The times are simulated.
128 devices in a mesh: gx: 16 (over y_hi, z, core), gy: 8 (over x, y_lo).
Axes of the slice: x: 4, y: 4 (y_hi: 2, y_lo: 2; y = y_hi * 2 + y_lo), z: 4, core: 2. Of those that a mesh axis runs over, the one named last changes fastest.
Arguments:
- mesh_state: bfloat16 [256, 256, 32, 128], P('gx', 'gy'), may hold values from -6 to 6
- part_feat: bfloat16 [524288, 128], P(('gx', 'gy')), may hold values from -6 to 6
- cell_index: int32 [524288], P(('gx', 'gy')), may hold values from 0 to 16383, as said below
- pairs: int32 [2, 3145728], P(None, ('gx', 'gy')), may hold values from 0 to 4095, as said below
- dest: int32 [524288], P(('gx', 'gy')), may hold values from 0 to 8, as said below
- mass: float32 [524288], P(('gx', 'gy')), may hold values from 0.5 to 2
- velocity: float32 [3, 524288], P(None, ('gx', 'gy')), may hold values from -30 to 30
- w_enc: bfloat16 [128, 128], replicated, may hold values from -0.5 to 0.5
- w_mesh: bfloat16 [128, 128], replicated, may hold values from -0.21875 to 0.21875
- w_pair: bfloat16 [128, 256], replicated, may hold values from -0.5 to 0.5
- w_edge: bfloat16 [128, 128], replicated, may hold values from -0.5 to 0.5
- w_node: bfloat16 [256, 128], replicated, may hold values from -0.25 to 0.25
- w_accel: bfloat16 [3, 128], replicated, may hold values from -0.5 to 0.5
Outputs:
- mesh_out: bfloat16 [256, 256, 32, 128], P('gx', 'gy')
- stay_feat: bfloat16 [524288, 128], P(('gx', 'gy'))
- stay_vel: float32 [3, 524288], P(None, ('gx', 'gy'))
- arrived_feat: bfloat16 [131072, 128], P(('gx', 'gy'))
- arrived_vel: float32 [4, 131072], P(None, ('gx', 'gy'))
Inputs may be any that keep to these rules, and one draw needn't show every extreme that they name: `dest`: 0 means the particle stays; k from 1 to 8 moves it in the k-th direction of the steps. At most 128 particles of one device take any one direction, and some device receives 128 particles from each of its eight neighbours. `cell_index`: A device's particles come in 8 aligned groups of 512 rows; the particles of group g lie in cells g * 2048 to (g + 1) * 2048 - 1 of the device's block. `pairs`: A device's columns come in 8 aligned groups of 3072; both rows of a column of group g name particles of the device's group g, rows g * 512 to (g + 1) * 512 - 1.
All inputs are finite; a program needn't handle non-finite values.
Results may differ from a plain program's by a relative error of at most 0.0085.
Values may be sent and summed in bfloat16 or wider, within the bound.
No kernel may reach another device: no remote copies, remote signals or barrier semaphores. Data moves between devices by JAX's collectives and lax.ppermute only.
A program may use at most 128 MiB of HBM per device.

v0:
```python
import jax
import jax.numpy as jnp
from jax import lax
from jax.sharding import Mesh
from jax.sharding import PartitionSpec as P

GX_GY = ("gx_0", "gx_1", "gx_2", "gy_0", "gy_1")
GX = ("gx_0", "gx_1", "gx_2")
GY = ("gy_0", "gy_1")


directions = ((-1, -1), (-1, 0), (-1, 1), (0, -1), (0, 1), (1, -1), (1, 0), (1, 1))


def extended(array, sides, width):
    edges = {}
    for axis, dim in sides:
        devices, length = (lax.axis_size(axis), array.shape[dim])
        up = [(i, (i + 1) % devices) for i in range(devices)]
        last = lax.slice_in_dim(array, length - width, length, axis=dim)
        initial = lax.slice_in_dim(array, 0, width, axis=dim)
        edges[dim] = (
            lax.ppermute(last, axis, up),
            lax.ppermute(initial, axis, [(b, a) for a, b in up]),
        )
    done = []
    for _, dim in sides:
        low, high = edges[dim]
        around = [(width, width) if d in done else (0, 0) for d in range(array.ndim)]
        array = jnp.concatenate([jnp.pad(low, around), array, jnp.pad(high, around)], axis=dim)
        done.append(dim)
    return array


def over_axes(array, axes):
    for axis in axes:
        array = lax.psum(array, axis)
    return array


def from_behind(block, axis, distance):
    devices = range(lax.axis_size(axis))
    route = [((i - distance) % len(devices), i) for i in devices]
    return lax.ppermute(block, axis, route)


def group_sizes(parts, cells):
    members = min(512, parts)
    count = parts // members
    return (members, count, cells // count)


def encode(state_rows, feat, cell, w_enc):
    members, count, span = group_sizes(feat.shape[0], state_rows.shape[0])
    width = feat.shape[1]
    feat_g = feat.reshape(count, members, width)
    cell_g = cell.reshape(count, members)
    lanes = jnp.arange(span, dtype=jnp.int32)

    def encode_one_group(item):
        rows, cells, number = item
        onehot = ((cells - number * span)[:, None] == lanes[None, :]).astype(jnp.bfloat16)
        return lax.dot_general(
            onehot, rows, (((0,), (0,)), ((), ())), preferred_element_type=jnp.float32
        )

    numbers = jnp.arange(count, dtype=jnp.int32)
    deposit = (
        lax.map(encode_one_group, (feat_g, cell_g, numbers)).reshape(-1, width).astype(jnp.bfloat16)
    )
    return (
        state_rows.astype(jnp.float32) + jnp.dot(deposit, w_enc, preferred_element_type=jnp.float32)
    ).astype(jnp.bfloat16)


def zsides(field):
    padded = jnp.pad(field, [(0, 0)] * (field.ndim - 2) + [(1, 1), (0, 0)])
    return padded[..., 2:, :] + padded[..., :-2, :]


def mesh_update(centre, sides, w_mesh):
    width = centre.shape[-1]
    summed = sides.astype(jnp.bfloat16).reshape(-1, width)
    update = jnp.dot(summed, w_mesh, preferred_element_type=jnp.float32).reshape(centre.shape)
    return (centre.astype(jnp.float32) + jax.nn.silu(update)).astype(jnp.bfloat16)


def particle_step(feat, cell, pair, mesh_rows, w_pair, w_edge, w_node):
    width = feat.shape[1]
    channels = mesh_rows.shape[1]
    members, count, span = group_sizes(feat.shape[0], mesh_rows.shape[0])
    proj = jnp.dot(feat, w_pair, preferred_element_type=jnp.float32).astype(jnp.bfloat16)
    per_group = pair.shape[1] // count
    proj_g = proj.reshape(count, members, 2 * width)
    feat_g = feat.reshape(count, members, width)
    pair_g = pair.reshape(2, count, per_group).transpose(1, 0, 2)
    cell_g = cell.reshape(count, members)
    rows_g = mesh_rows.reshape(count, span, channels)
    lanes = jnp.arange(members, dtype=jnp.int32)
    cell_lanes = jnp.arange(span, dtype=jnp.int32)

    def particle_one_group(carry, item):
        proj_part, feat_part, pair_part, cell_part, mesh_part, number = item
        base = number * members
        send_hot = ((pair_part[0] - base)[:, None] == lanes[None, :]).astype(jnp.bfloat16)
        recv_hot = ((pair_part[1] - base)[:, None] == lanes[None, :]).astype(jnp.bfloat16)
        sent = jnp.dot(send_hot, proj_part[:, :width], preferred_element_type=jnp.float32)
        received = jnp.dot(recv_hot, proj_part[:, width:], preferred_element_type=jnp.float32)
        act = jax.nn.silu(sent + received).astype(jnp.bfloat16)
        message = jnp.dot(act, w_edge, preferred_element_type=jnp.float32)
        edge_sum = lax.dot_general(
            recv_hot.astype(jnp.float32),
            message,
            (((0,), (0,)), ((), ())),
            preferred_element_type=jnp.float32,
        )
        edge_sum = edge_sum.astype(jnp.bfloat16)
        cell_hot = ((cell_part - number * span)[:, None] == cell_lanes[None, :]).astype(
            jnp.bfloat16
        )
        near = jnp.dot(cell_hot, mesh_part, preferred_element_type=jnp.float32).astype(jnp.bfloat16)
        update = jnp.dot(edge_sum, w_node[:width], preferred_element_type=jnp.float32)
        update = update + jnp.dot(near, w_node[width:], preferred_element_type=jnp.float32)
        return (carry, (feat_part.astype(jnp.float32) + jax.nn.silu(update)).astype(jnp.bfloat16))

    numbers = jnp.arange(count, dtype=jnp.int32)
    _, h_groups = lax.scan(particle_one_group, 0, (proj_g, feat_g, pair_g, cell_g, rows_g, numbers))
    return h_groups.reshape(-1, width)


def pack(h_new, vel1, mass, dest, cap):
    ways = jnp.arange(1, 9, dtype=jnp.int32)
    onehot = (dest[:, None] == ways[None, :]).astype(jnp.int32)
    slot = jnp.sum((jnp.cumsum(onehot, axis=0) - 1) * onehot, axis=1)
    extra = jnp.concatenate([vel1, mass[None, :]], axis=0).astype(jnp.bfloat16)
    slots = jnp.arange(cap, dtype=jnp.int32)
    feats = []
    moving = []
    for way in range(1, 9):
        chosen = ((dest == way)[None, :] & (slot[None, :] == slots[:, None])).astype(jnp.bfloat16)
        feats.append(
            jnp.dot(chosen, h_new, preferred_element_type=jnp.float32).astype(jnp.bfloat16)
        )
        moving.append(
            lax.dot_general(
                extra, chosen, (((1,), (1,)), ((), ())), preferred_element_type=jnp.float32
            ).astype(jnp.bfloat16)
        )
    return (jnp.stack(feats, axis=0), jnp.stack(moving, axis=0))


def unpack(moving, drift):
    values = moving.astype(jnp.float32)
    weight = values[..., 3:4, :]
    speed = jnp.where(weight > 0, values[..., :3, :] - drift[:, None], 0.0)
    return jnp.concatenate([speed, weight], axis=-2)


def shards(
    mesh_state,
    part_feat,
    cell_index,
    pairs,
    dest,
    mass,
    velocity,
    w_enc,
    w_mesh,
    w_pair,
    w_edge,
    w_node,
    w_accel,
):
    shape = mesh_state.shape
    width = part_feat.shape[1]
    mesh1 = encode(mesh_state.reshape(-1, shape[3]), part_feat, cell_index, w_enc).reshape(shape)
    padded = extended(mesh1, ((GX, 0), (GY, 1)), 1)
    wide = padded.astype(jnp.float32)
    centre = wide[1:-1, 1:-1]
    sides = wide[:-2, 1:-1] + wide[2:, 1:-1] + wide[1:-1, :-2] + wide[1:-1, 2:] + zsides(centre)
    mesh2 = mesh_update(mesh1, sides, w_mesh)
    h_new = particle_step(
        part_feat, cell_index, pairs, mesh2.reshape(-1, shape[3]), w_pair, w_edge, w_node
    )
    accel = lax.dot_general(
        w_accel, h_new, (((1,), (1,)), ((), ())), preferred_element_type=jnp.float32
    )
    vel1 = velocity + accel
    momentum, total_mass = (
        over_axes(jnp.sum(mass[None, :] * vel1, axis=1), GX_GY),
        over_axes(jnp.sum(mass), GX_GY),
    )
    drift = momentum / total_mass
    staying = dest == 0
    stay_feat = jnp.where(staying[:, None], h_new, jnp.zeros_like(h_new))
    stay_vel = jnp.where(staying[None, :], vel1 - drift[:, None], 0.0)
    cap = part_feat.shape[0] // 32
    feats, moving = pack(h_new, vel1, mass, dest, cap)
    got_f = [feats[k] for k in range(8)]
    got_m = [moving[k] for k in range(8)]
    for step_x in (1, -1):
        chosen = [k for k, offset in enumerate(directions) if offset[0] == step_x]
        moved_f, moved_m = from_behind(
            (
                jnp.stack([got_f[k] for k in chosen], axis=0),
                jnp.stack([got_m[k] for k in chosen], axis=0),
            ),
            GX,
            step_x,
        )
        for place, k in enumerate(chosen):
            got_f[k] = moved_f[place]
            got_m[k] = moved_m[place]
    for step_y in (1, -1):
        chosen = [k for k, offset in enumerate(directions) if offset[1] == step_y]
        moved_f, moved_m = from_behind(
            (
                jnp.stack([got_f[k] for k in chosen], axis=0),
                jnp.stack([got_m[k] for k in chosen], axis=0),
            ),
            GY,
            step_y,
        )
        for place, k in enumerate(chosen):
            got_f[k] = moved_f[place]
            got_m[k] = moved_m[place]
    arrived_f = jnp.stack(got_f, axis=0)
    arrived_m = jnp.stack(got_m, axis=0)
    arrived_feat = arrived_f.reshape(-1, width)
    arrived_vel = unpack(arrived_m, drift).transpose(1, 0, 2).reshape(4, -1)
    return (mesh2, stay_feat, stay_vel, arrived_feat, arrived_vel)


def solution(mesh):
    torus = Mesh(mesh.devices.reshape(2, 4, 2, 4, 2), ("gx_0", "gx_1", "gx_2", "gy_0", "gy_1"))
    placed = (
        P(GX, GY, None, None),
        P(GX_GY, None),
        P(GX_GY),
        P(None, GX_GY),
        P(GX_GY),
        P(GX_GY),
        P(None, GX_GY),
        P(),
        P(),
        P(),
        P(),
        P(),
        P(),
    )
    return jax.shard_map(
        shards,
        mesh=torus,
        in_specs=placed,
        out_specs=(
            P(GX, GY, None, None),
            P(GX_GY, None),
            P(None, GX_GY),
            P(GX_GY, None),
            P(None, GX_GY),
        ),
        check_vma=False,
    )
```

profile of v0, /device:TPU:0, one launch (start us, length us, event | category | flops | bytes accessed | tf_op | source)
XLA Modules:
  0.0 295.2 jit_solution(16793231699524148974)
XLA Ops:
  1.4 34.5 %while.23 = (s32[]{:T(128)}, bf16[8,2048,128]{2,1,0:T(8,128)(2,1)}, s32[8,512]{1,0:T(8,128)S(1)}, s32[8]{0:T(128)S(1)}, bf16[8,512,128]{2,1,0:T(8,128)(2,1)}, /*index=5*/s32[]{:T(128)}, s32[1]{0:T(128)}) while((s32[]{:T(128)}, bf16[8,2048,128]{2,1,0:T(8,128)(2,1)}, s32[8,512]{1,0:T(8,128)S(1)}, s32[8]{0:T(128)S(1)}, ...), condition=%wide.region_1.2_spmd.clone, body=%wide.region_0.1_spmd.clone.sunk | while | flops 269484544 | bytes 1186925 | solution.py:69
  35.9 4.8 %fusion.48 = bf16[16384,128]{1,0:T(8,128)(2,1)S(1)} fusion(bf16[16384,128]{1,0:T(8,128)(2,1)} %bitcast.173, bf16[128,128]{1,0:T(8,128)(2,1)S(1)} %copy-done.9, bf16[16384,128]{1,0:T(8,128)(2,1)} %bitcast.172), kind=kOutput, calls=%fused_computation.46 | convolution fusion | flops 543162368 | bytes 12615680 | tf_op jit(solution)/shard_map/dot_general | solution.py:72
  46.4 5.7 %collective-permute-start.2 = (bf16[1,32,32,128]{3,2,1,0:T(8,128)(2,1)}, bf16[1,32,32,128]{3,2,1,0:T(8,128)(2,1)}, u32[]{:S(2)}, u32[]{:S(2)}) collective-permute-start(bf16[1,32,32,128]{3,2,1,0:T(8,128)(2,1)} %bitcast.5), channel_id=1, source_target_pairs={{8,0},{16,8},{24,16},{32,24},{40,32},{48,40},{56,48},{64,56},{72,6... | collective-permute-start | bytes 786440 | tf_op jit(solution)/shard_map/ppermute | solution.py:24
  58.7 3.9 %fusion.55 = f32[18,34,32,128]{3,2,1,0:T(8,128)S(1)} fusion(bf16[16,1,32,128]{3,2,1,0:T(8,128)(2,1)} %collective-permute-done.3, bf16[16,1,32,128]{3,2,1,0:T(8,128)(2,1)} %collective-permute-done, bf16[1,32,32,128]{3,2,1,0:T(8,128)(2,1)} %collective-permute-done.2, bf16[16,32,32,128]{3,2,1,0:T(8,128)(2,1)} %bitcast.170, ...), kind=kLoop, calls=%fused_computation.62 | loop fusion | flops 35094528 | bytes 15007744 | tf_op jit(solution)/shard_map/convert_element_type | solution.py:178
  62.6 3.8 %copy-done.1 = f32[18,34,32,128]{3,2,1,0:T(8,128)} copy-done((f32[18,34,32,128]{3,2,1,0:T(8,128)}, f32[18,34,32,128]{3,2,1,0:T(8,128)S(1)}, u32[]{:S(2)}) %copy-start.1) | copy-done | bytes 10027032
  66.4 4.4 %slice.206 = f32[16,32,32,128]{3,2,1,0:T(8,128)} slice(f32[18,34,32,128]{3,2,1,0:T(8,128)S(1)} %fusion.55), slice={[1:17], [1:33], [0:32], [0:128]} | slice | bytes 16777216 | tf_op jit(solution)/shard_map/slice | solution.py:179
  70.8 19.6 %add_convert_fusion = bf16[16,32,32,128]{3,2,1,0:T(8,128)(2,1)} fusion(bf16[16,32,32,128]{3,2,1,0:T(8,128)(2,1)S(1)} %bitcast.171, f32[16,32,32,128]{3,2,1,0:T(8,128)} %slice.206, f32[18,34,32,128]{3,2,1,0:T(8,128)} %copy-done.1, bf16[128,128]{1,0:T(8,128)(2,1)S(1)} %copy-done.19), kind=kOutput, calls=%fused_computation.59 | convolution fusion | flops 564133888 | bytes 50364416 | tf_op jit(solution)/shard_map/dot_general | solution.py:84
  90.9 119.2 %while.24 = (s32[]{:T(128)}, bf16[8,512,128]{2,1,0:T(8,128)(2,1)S(1)}, bf16[8,512,128]{2,1,0:T(8,128)(2,1)}, s32[8,2,3072]{2,1,0:T(2,128)}, s32[8]{0:T(128)}, /*...) while((s32[]{:T(128)}, ...), condition=%wide.region_3.4_spmd.clone.clone, body=%wide.region_2.3_spmd.clone.clone.sunk | while | flops 1619401216 | bytes 7269589 | solution.py:127
  97.3 4.1 %fusion.295 = bf16[512,128]{1,0:T(8,128)(2,1)} fusion(bf16[3072,128]{1,0:T(8,128)(2,1)} %multiply_convert_fusion.2, bf16[128,128]{1,0:T(8,128)(2,1)} %get-tuple-element.389, s32[3072]{0:T(1024)S(1)} %bitcast.187), kind=kOutput, calls=%fused_computation.27.clone.1 | convolution fusion | flops 504954880 | bytes 962560 | tf_op jit(solution)/shard_map/while/body/eval_jaxpr/dot_general | solution.py:111
  112.2 4.1 %fusion.295 = bf16[512,128]{1,0:T(8,128)(2,1)} fusion(bf16[3072,128]{1,0:T(8,128)(2,1)} %multiply_convert_fusion.2, bf16[128,128]{1,0:T(8,128)(2,1)} %get-tuple-element.389, s32[3072]{0:T(1024)S(1)} %bitcast.187), kind=kOutput, calls=%fused_computation.27.clone.1 | convolution fusion | flops 504954880 | bytes 962560 | tf_op jit(solution)/shard_map/while/body/eval_jaxpr/dot_general | solution.py:111
  127.1 4.1 %fusion.295 = bf16[512,128]{1,0:T(8,128)(2,1)} fusion(bf16[3072,128]{1,0:T(8,128)(2,1)} %multiply_convert_fusion.2, bf16[128,128]{1,0:T(8,128)(2,1)} %get-tuple-element.389, s32[3072]{0:T(1024)S(1)} %bitcast.187), kind=kOutput, calls=%fused_computation.27.clone.1 | convolution fusion | flops 504954880 | bytes 962560 | tf_op jit(solution)/shard_map/while/body/eval_jaxpr/dot_general | solution.py:111
  142.0 4.1 %fusion.295 = bf16[512,128]{1,0:T(8,128)(2,1)} fusion(bf16[3072,128]{1,0:T(8,128)(2,1)} %multiply_convert_fusion.2, bf16[128,128]{1,0:T(8,128)(2,1)} %get-tuple-element.389, s32[3072]{0:T(1024)S(1)} %bitcast.187), kind=kOutput, calls=%fused_computation.27.clone.1 | convolution fusion | flops 504954880 | bytes 962560 | tf_op jit(solution)/shard_map/while/body/eval_jaxpr/dot_general | solution.py:111
  156.9 4.1 %fusion.295 = bf16[512,128]{1,0:T(8,128)(2,1)} fusion(bf16[3072,128]{1,0:T(8,128)(2,1)} %multiply_convert_fusion.2, bf16[128,128]{1,0:T(8,128)(2,1)} %get-tuple-element.389, s32[3072]{0:T(1024)S(1)} %bitcast.187), kind=kOutput, calls=%fused_computation.27.clone.1 | convolution fusion | flops 504954880 | bytes 962560 | tf_op jit(solution)/shard_map/while/body/eval_jaxpr/dot_general | solution.py:111
  171.8 4.1 %fusion.295 = bf16[512,128]{1,0:T(8,128)(2,1)} fusion(bf16[3072,128]{1,0:T(8,128)(2,1)} %multiply_convert_fusion.2, bf16[128,128]{1,0:T(8,128)(2,1)} %get-tuple-element.389, s32[3072]{0:T(1024)S(1)} %bitcast.187), kind=kOutput, calls=%fused_computation.27.clone.1 | convolution fusion | flops 504954880 | bytes 962560 | tf_op jit(solution)/shard_map/while/body/eval_jaxpr/dot_general | solution.py:111
  186.7 4.1 %fusion.295 = bf16[512,128]{1,0:T(8,128)(2,1)} fusion(bf16[3072,128]{1,0:T(8,128)(2,1)} %multiply_convert_fusion.2, bf16[128,128]{1,0:T(8,128)(2,1)} %get-tuple-element.389, s32[3072]{0:T(1024)S(1)} %bitcast.187), kind=kOutput, calls=%fused_computation.27.clone.1 | convolution fusion | flops 504954880 | bytes 962560 | tf_op jit(solution)/shard_map/while/body/eval_jaxpr/dot_general | solution.py:111
  201.6 4.1 %fusion.295 = bf16[512,128]{1,0:T(8,128)(2,1)} fusion(bf16[3072,128]{1,0:T(8,128)(2,1)} %multiply_convert_fusion.2, bf16[128,128]{1,0:T(8,128)(2,1)} %get-tuple-element.389, s32[3072]{0:T(1024)S(1)} %bitcast.187), kind=kOutput, calls=%fused_computation.27.clone.1 | convolution fusion | flops 504954880 | bytes 962560 | tf_op jit(solution)/shard_map/while/body/eval_jaxpr/dot_general | solution.py:111
  211.5 6.9 %all-reduce.7 = (f32[3]{0:T(128)S(1)}, f32[]{:T(128)}) all-reduce(f32[3]{0:T(128)S(1)} %get-tuple-element.234, f32[]{:T(128)} %get-tuple-element.220), channel_id=1, replica_groups=mesh['gx_0'=2,'gx_1'=4,'gx_2'=2,'gy_0'=4,'gy_1'=2] {'gx_0'}, use_global_device_ids=true, to_apply=%region_5.6 | all-reduce | flops 4 | bytes 32 | tf_op jit(solution)/shard_map/psum | solution.py:37
  218.5 8.4 %all-reduce.4 = (f32[3]{0:T(128)S(1)}, f32[]{:T(128)}) all-reduce(f32[3]{0:T(128)S(1)} %get-tuple-element.205, f32[]{:T(128)} %get-tuple-element.206), channel_id=1, replica_groups=mesh['gx_0'=2,'gx_1'=4,'gx_2'=2,'gy_0'=4,'gy_1'=2] {'gx_1'}, use_global_device_ids=true, to_apply=%region_6.7 | all-reduce | flops 4 | bytes 32 | tf_op jit(solution)/shard_map/psum | solution.py:37
  230.0 11.0 %all-reduce.3 = (f32[3]{0:T(128)S(1)}, f32[]{:T(128)}) all-reduce(f32[3]{0:T(128)S(1)} %get-tuple-element.203, f32[]{:T(128)} %get-tuple-element.204), channel_id=1, replica_groups=mesh['gx_0'=2,'gx_1'=4,'gx_2'=2,'gy_0'=4,'gy_1'=2] {'gy_0'}, use_global_device_ids=true, to_apply=%region_8.9 | all-reduce | flops 4 | bytes 32 | tf_op jit(solution)/shard_map/psum | solution.py:37
  241.0 5.8 %all-reduce.5 = (f32[3]{0:T(128)S(1)}, f32[]{:T(128)}) all-reduce(f32[3]{0:T(128)S(1)} %get-tuple-element.197, f32[]{:T(128)} %get-tuple-element.198), channel_id=1, replica_groups=mesh['gx_0'=2,'gx_1'=4,'gx_2'=2,'gy_0'=4,'gy_1'=2] {'gy_1'}, use_global_device_ids=true, to_apply=%region_9.10 | all-reduce | flops 4 | bytes 32 | tf_op jit(solution)/shard_map/psum | solution.py:37
  262.7 5.3 %collective-permute-start.8 = (bf16[3,4,128]{2,1,0:T(4,128)(2,1)S(1)}, bf16[3,4,128]{2,1,0:T(4,128)(2,1)S(1)}, u32[]{:S(2)}, u32[]{:S(2)}) collective-permute-start(bf16[3,4,128]{2,1,0:T(4,128)(2,1)S(1)} %pad_maximum_fusion.5), channel_id=1, source_target_pairs={{8,0},{16,8},{24,16},{32,24},{40,32},{48,40},{56,48},{64,56},{72,6... | collective-permute-start | bytes 9224 | tf_op jit(solution)/shard_map/ppermute | solution.py:44
  275.0 4.6 %collective-permute-start.4 = (bf16[3,128,128]{2,1,0:T(8,128)(2,1)S(1)}, bf16[3,128,128]{2,1,0:T(8,128)(2,1)S(1)}, u32[]{:S(2)}, u32[]{:S(2)}) collective-permute-start(bf16[3,128,128]{2,1,0:T(8,128)(2,1)S(1)} %pad_maximum_fusion), channel_id=1, source_target_pairs={{8,0},{16,8},{24,16},{32,24},{40,32},{48,40},{56,48},{64,56},{72,6... | collective-permute-start | bytes 294920 | tf_op jit(solution)/shard_map/ppermute | solution.py:44
  283.0 4.6 %collective-permute-done.6 = bf16[3,128,128]{2,1,0:T(8,128)(2,1)S(1)} collective-permute-done((bf16[3,128,128]{2,1,0:T(8,128)(2,1)S(1)}, bf16[3,128,128]{2,1,0:T(8,128)(2,1)S(1)}, u32[]{:S(2)}, u32[]{:S(2)}) %collective-permute-start.6) | collective-permute-done | bytes 98336 | tf_op jit(solution)/shard_map/ppermute | solution.py:44
  288.3 6.1 %collective-permute-done.7 = bf16[3,128,128]{2,1,0:T(8,128)(2,1)S(1)} collective-permute-done((bf16[3,128,128]{2,1,0:T(8,128)(2,1)S(1)}, bf16[3,128,128]{2,1,0:T(8,128)(2,1)S(1)}, u32[]{:S(2)}, u32[]{:S(2)}) %collective-permute-start.7) | collective-permute-done | bytes 98336 | tf_op jit(solution)/shard_map/ppermute | solution.py:44
  (220 shorter events, 150.8 us)
Async XLA Ops:
  0.6 51.5 %copy-start = (bf16[128,256]{1,0:T(8,128)(2,1)S(1)}, bf16[128,256]{1,0:T(8,128)(2,1)}, u32[]{:S(2)}) copy-start(bf16[128,256]{1,0:T(8,128)(2,1)} %param.26) | copy-start | bytes 196612
  1.4 34.5 %copy-start.9 = (bf16[128,128]{1,0:T(8,128)(2,1)S(1)}, bf16[128,128]{1,0:T(8,128)(2,1)}, u32[]{:S(2)}) copy-start(bf16[128,128]{1,0:T(8,128)(2,1)} %param.24) | copy-start | bytes 98308
  35.9 16.2 %copy-start.4 = (bf16[8,512,128]{2,1,0:T(8,128)(2,1)S(1)}, bf16[8,512,128]{2,1,0:T(8,128)(2,1)}, u32[]{:S(2)}) copy-start(bf16[8,512,128]{2,1,0:T(8,128)(2,1)} %get-tuple-element.398) | copy-start | bytes 3145732
  40.7 4.9 %copy-start.2 = (bf16[16384,128]{1,0:T(8,128)(2,1)}, bf16[16384,128]{1,0:T(8,128)(2,1)S(1)}, u32[]{:S(2)}) copy-start(bf16[16384,128]{1,0:T(8,128)(2,1)S(1)} %fusion.48) | copy-start | bytes 12582916
  40.7 12.1 %copy-start.6 = (s32[4096]{0:T(1024)S(1)}, s32[4096]{0:T(1024)}, u32[]{:S(2)}) copy-start(s32[4096]{0:T(1024)} %param.21) | copy-start | bytes 49156
  40.8 15.7 %copy-start.7 = (f32[4096]{0:T(1024)S(1)}, f32[4096]{0:T(1024)}, u32[]{:S(2)}) copy-start(f32[4096]{0:T(1024)} %param.22) | copy-start | bytes 49156
  41.5 17.0 %collective-permute-start = (bf16[16,1,32,128]{3,2,1,0:T(8,128)(2,1)}, bf16[16,1,32,128]{3,2,1,0:T(8,128)(2,1)}, u32[]{:S(2)}, u32[]{:S(2)}) collective-permute-start(bf16[16,1,32,128]{3,2,1,0:T(8,128)(2,1)} %get-tuple-element.211), channel_id=1, source_target_pairs={{0,1},{1,2},{2,3},{3,4},{4,5},{5,6},{6,7},{7,0},{8,9},{9,10},{10,1... | collective-permute-start | bytes 393224 | tf_op jit(solution)/shard_map/ppermute | solution.py:23
  43.2 15.3 %collective-permute-start.3 = (bf16[16,1,32,128]{3,2,1,0:T(8,128)(2,1)}, bf16[16,1,32,128]{3,2,1,0:T(8,128)(2,1)}, u32[]{:S(2)}, u32[]{:S(2)}) collective-permute-start(bf16[16,1,32,128]{3,2,1,0:T(8,128)(2,1)} %get-tuple-element.212), channel_id=1, source_target_pairs={{1,0},{2,1},{3,2},{4,3},{5,4},{6,5},{7,6},{0,7},{9,8},{10,9},{11,1... | collective-permute-start | bytes 393224 | tf_op jit(solution)/shard_map/ppermute | solution.py:24
  46.4 12.2 %collective-permute-start.1 = (bf16[1,32,32,128]{3,2,1,0:T(8,128)(2,1)}, bf16[1,32,32,128]{3,2,1,0:T(8,128)(2,1)}, u32[]{:S(2)}, u32[]{:S(2)}) collective-permute-start(bf16[1,32,32,128]{3,2,1,0:T(8,128)(2,1)} %bitcast.4), channel_id=1, source_target_pairs={{0,8},{8,16},{16,24},{24,32},{32,40},{40,48},{48,56},{56,64},{64,7... | collective-permute-start | bytes 786440 | tf_op jit(solution)/shard_map/ppermute | solution.py:23
  46.4 12.2 %collective-permute-start.2 = (bf16[1,32,32,128]{3,2,1,0:T(8,128)(2,1)}, bf16[1,32,32,128]{3,2,1,0:T(8,128)(2,1)}, u32[]{:S(2)}, u32[]{:S(2)}) collective-permute-start(bf16[1,32,32,128]{3,2,1,0:T(8,128)(2,1)} %bitcast.5), channel_id=1, source_target_pairs={{8,0},{16,8},{24,16},{32,24},{40,32},{48,40},{56,48},{64,56},{72,6... | collective-permute-start | bytes 786440 | tf_op jit(solution)/shard_map/ppermute | solution.py:24
  66.4 4.4 %copy-start.19 = (bf16[128,128]{1,0:T(8,128)(2,1)S(1)}, bf16[128,128]{1,0:T(8,128)(2,1)}, u32[]{:S(2)}) copy-start(bf16[128,128]{1,0:T(8,128)(2,1)} %param.25) | copy-start | bytes 98308
  70.8 20.1 %copy-start.5 = (bf16[256,128]{1,0:T(8,128)(2,1)S(1)}, bf16[256,128]{1,0:T(8,128)(2,1)}, u32[]{:S(2)}) copy-start(bf16[256,128]{1,0:T(8,128)(2,1)} %param.28) | copy-start | bytes 196612
  210.1 42.0 %copy-start.10 = (s32[4096]{0:T(1024)S(1)}, s32[4096]{0:T(1024)}, u32[]{:S(2)}) copy-start(s32[4096]{0:T(1024)} %fusion.231) | copy-start | bytes 49156
  210.1 42.0 %copy-start.18 = (pred[4096]{0:T(1024)(128)(4,1)S(1)}, pred[4096]{0:T(1024)(128)(4,1)}, u32[]{:S(2)}) copy-start(pred[4096]{0:T(1024)(128)(4,1)} %get-tuple-element.222) | copy-start | bytes 12292
  210.2 43.0 %copy-start.17 = (pred[4096]{0:T(1024)(128)(4,1)S(1)}, pred[4096]{0:T(1024)(128)(4,1)}, u32[]{:S(2)}) copy-start(pred[4096]{0:T(1024)(128)(4,1)} %get-tuple-element.229) | copy-start | bytes 12292
  249.6 4.7 %copy-start.16 = (pred[4096]{0:T(1024)(128)(4,1)S(1)}, pred[4096]{0:T(1024)(128)(4,1)}, u32[]{:S(2)}) copy-start(pred[4096]{0:T(1024)(128)(4,1)} %get-tuple-element.227) | copy-start | bytes 12292
  262.6 6.6 %collective-permute-start.9 = (bf16[3,4,128]{2,1,0:T(4,128)(2,1)S(1)}, bf16[3,4,128]{2,1,0:T(4,128)(2,1)S(1)}, u32[]{:S(2)}, u32[]{:S(2)}) collective-permute-start(bf16[3,4,128]{2,1,0:T(4,128)(2,1)S(1)} %pad_maximum_fusion.6), channel_id=1, source_target_pairs={{120,0},{0,8},{8,16},{16,24},{24,32},{32,40},{40,48},{48,56},{56,6... | collective-permute-start | bytes 9224 | tf_op jit(solution)/shard_map/ppermute | solution.py:44
  262.7 6.7 %collective-permute-start.8 = (bf16[3,4,128]{2,1,0:T(4,128)(2,1)S(1)}, bf16[3,4,128]{2,1,0:T(4,128)(2,1)S(1)}, u32[]{:S(2)}, u32[]{:S(2)}) collective-permute-start(bf16[3,4,128]{2,1,0:T(4,128)(2,1)S(1)} %pad_maximum_fusion.5), channel_id=1, source_target_pairs={{8,0},{16,8},{24,16},{32,24},{40,32},{48,40},{56,48},{64,56},{72,6... | collective-permute-start | bytes 9224 | tf_op jit(solution)/shard_map/ppermute | solution.py:44
  269.3 3.7 %collective-permute-start.10 = (bf16[3,4,128]{2,1,0:T(4,128)(2,1)S(1)}, bf16[3,4,128]{2,1,0:T(4,128)(2,1)S(1)}, u32[]{:S(2)}, u32[]{:S(2)}) collective-permute-start(bf16[3,4,128]{2,1,0:T(4,128)(2,1)S(1)} %pad_maximum_fusion.7), channel_id=1, source_target_pairs={{1,0},{2,1},{3,2},{4,3},{5,4},{6,5},{7,6},{0,7},{9,8},{10,9},{11,1... | collective-permute-start | bytes 9224 | tf_op jit(solution)/shard_map/ppermute | solution.py:44
  269.6 10.1 %collective-permute-start.5 = (bf16[3,128,128]{2,1,0:T(8,128)(2,1)S(1)}, bf16[3,128,128]{2,1,0:T(8,128)(2,1)S(1)}, u32[]{:S(2)}, u32[]{:S(2)}) collective-permute-start(bf16[3,128,128]{2,1,0:T(8,128)(2,1)S(1)} %pad_maximum_fusion.1), channel_id=1, source_target_pairs={{120,0},{0,8},{8,16},{16,24},{24,32},{32,40},{40,48},{48,56},{56,6... | collective-permute-start | bytes 294920 | tf_op jit(solution)/shard_map/ppermute | solution.py:44
  273.0 6.6 %collective-permute-start.11 = (bf16[3,4,128]{2,1,0:T(4,128)(2,1)S(1)}, bf16[3,4,128]{2,1,0:T(4,128)(2,1)S(1)}, u32[]{:S(2)}, u32[]{:S(2)}) collective-permute-start(bf16[3,4,128]{2,1,0:T(4,128)(2,1)S(1)} %pad_maximum_fusion.8), channel_id=1, source_target_pairs={{7,0},{0,1},{1,2},{2,3},{3,4},{4,5},{5,6},{6,7},{15,8},{8,9},{9,10... | collective-permute-start | bytes 9224 | tf_op jit(solution)/shard_map/ppermute | solution.py:44
  275.0 7.0 %collective-permute-start.4 = (bf16[3,128,128]{2,1,0:T(8,128)(2,1)S(1)}, bf16[3,128,128]{2,1,0:T(8,128)(2,1)S(1)}, u32[]{:S(2)}, u32[]{:S(2)}) collective-permute-start(bf16[3,128,128]{2,1,0:T(8,128)(2,1)S(1)} %pad_maximum_fusion), channel_id=1, source_target_pairs={{8,0},{16,8},{24,16},{32,24},{40,32},{48,40},{56,48},{64,56},{72,6... | collective-permute-start | bytes 294920 | tf_op jit(solution)/shard_map/ppermute | solution.py:44
  282.0 5.6 %collective-permute-start.6 = (bf16[3,128,128]{2,1,0:T(8,128)(2,1)S(1)}, bf16[3,128,128]{2,1,0:T(8,128)(2,1)S(1)}, u32[]{:S(2)}, u32[]{:S(2)}) collective-permute-start(bf16[3,128,128]{2,1,0:T(8,128)(2,1)S(1)} %pad_maximum_fusion.2), channel_id=1, source_target_pairs={{1,0},{2,1},{3,2},{4,3},{5,4},{6,5},{7,6},{0,7},{9,8},{10,9},{11,1... | collective-permute-start | bytes 294920 | tf_op jit(solution)/shard_map/ppermute | solution.py:44
  287.6 6.8 %collective-permute-start.7 = (bf16[3,128,128]{2,1,0:T(8,128)(2,1)S(1)}, bf16[3,128,128]{2,1,0:T(8,128)(2,1)S(1)}, u32[]{:S(2)}, u32[]{:S(2)}) collective-permute-start(bf16[3,128,128]{2,1,0:T(8,128)(2,1)S(1)} %pad_maximum_fusion.3), channel_id=1, source_target_pairs={{7,0},{0,1},{1,2},{2,3},{3,4},{4,5},{5,6},{6,7},{15,8},{8,9},{9,10... | collective-permute-start | bytes 294920 | tf_op jit(solution)/shard_map/ppermute | solution.py:44
  (8 other events, 22.8 us)
where the time goes:
time: 297 us; the launch traced here: 295 us
  matrix products  148 us (50%)
  blocking collectives  35.2 us (12%)
  local copies, waits for them, and re-layouts  27 us (9%)
  other arithmetic  26.6 us (9%)
  starting transfers between devices  23 us (8%)
  waiting for transfers between devices  17.8 us (6%)
  loops' own time  16.1 us (5%)
    psum x5, blocking collectives, over_axes(): array = lax.psum(array, axis)  35.2 us
    dot_general x8, matrix products, particle_one_group(): lax.dot_general(recv_hot.astype(jnp.float32), message, (((0,), (0,)), (()...  32.5 us
    dot_general x8, matrix products, encode_one_group(): lax.dot_general(onehot, rows, (((0,), (0,)), ((), ())), preferred_element...  24.5 us
    dot_general x8, matrix products, particle_one_group(): jnp.dot(send_hot, proj_part[:, :width], preferred_element_type=jnp.float32)  20.9 us
    dot_general x1, matrix products, mesh_update(): jnp.dot(summed, w_mesh, preferred_element_type=jnp.float32)  19.6 us
    ppermute x8, waiting for transfers between devices, from_behind(): return lax.ppermute(block, axis, route)  17.6 us
    dot_general x8, matrix products, particle_one_group(): jnp.dot(near, w_node[width:], preferred_element_type=jnp.float32)  17 us
    dynamic_slice x16, local copies, waits for them, and re-layouts, encode(): lax.map(encode_one_group, (feat_g, cell_g, numbers)).reshape(-1, width)  13.9 us
  transfers between devices with their start and end apart: 12, of which 6 were waited for; matrix products, arithmetic and copies ran while one was open for 3% of the time, Pallas kernels for 0%

commit v1 on v0

v1 whole, which is shorter than its diff:
```python
import jax
import jax.numpy as jnp
from jax import lax
from jax.experimental import pallas as pl
from jax.experimental.pallas import tpu as pltpu
from jax.sharding import Mesh
from jax.sharding import PartitionSpec as P

GX_GY = ("gx_0", "gx_1", "gx_2", "gy_0", "gy_1")
GX = ("gx_0", "gx_1", "gx_2")
GY = ("gy_0", "gy_1")

DIRECTIONS = ((-1, -1), (-1, 0), (-1, 1), (0, -1), (0, 1), (1, -1), (1, 0), (1, 1))

F = 128
GRP = 512
NGRP = 8
PLANE = 1024
SPAN = 2 * PLANE
EDGES = 3072
HALF = 256
CAP = 128
SENT = 144
ECHUNK = 512

bf16 = jnp.bfloat16
f32 = jnp.float32


def dot(a, b):
    return jnp.dot(a, b, preferred_element_type=f32)


def dot_nt(a, b):
    return lax.dot_general(a, b, (((1,), (1,)), ((), ())), preferred_element_type=f32)


def silu(v):
    half = 0.5 * v
    return half + half * jnp.tanh(half)


def one_hot(rows, index):
    lanes = index.shape[1]
    return jnp.where(lax.broadcasted_iota(jnp.int32, (rows, lanes), 0) == index, 1.0, 0.0).astype(bf16)


def encode_kernel(state, feat, cell, w_enc, mesh1, y_low, y_high, x_low, x_high):
    g = pl.program_id(0)
    local = cell[0] - g * SPAN
    row = local & (PLANE - 1)
    plane = (local >> 10).astype(f32)
    upper = jnp.transpose(jnp.broadcast_to(plane, (8, GRP)))[:, 0:1]
    rows = feat[...].astype(f32)
    spread = jnp.concatenate([(rows * (1.0 - upper)).astype(bf16), (rows * upper).astype(bf16)], axis=1)
    chunk = 256
    for at in range(0, PLANE, chunk):
        hot = one_hot(chunk, row - at)
        deposit = dot(hot, spread).astype(bf16)
        for p in range(2):
            here = pl.ds(p * PLANE + at, chunk)
            mesh1[here, :] = (
                state[here, :].astype(f32) + dot(deposit[:, p * F : (p + 1) * F], w_enc[...])
            ).astype(bf16)
    for p in range(2):
        y_low[p] = mesh1[pl.ds(p * PLANE, 32), :]
        y_high[p] = mesh1[pl.ds(p * PLANE + PLANE - 32, 32), :]

    @pl.when(g == 0)
    def _():
        x_low[...] = mesh1[pl.ds(0, PLANE), :]

    @pl.when(g == NGRP - 1)
    def _():
        x_high[...] = mesh1[pl.ds(PLANE, PLANE), :]


def encode(state, feat, cell3, w_enc):
    full = lambda g: (0, 0)
    part = lambda g: (g, 0)
    return pl.pallas_call(
        encode_kernel,
        grid=(NGRP,),
        in_specs=[
            pl.BlockSpec((SPAN, F), part),
            pl.BlockSpec((GRP, F), part),
            pl.BlockSpec((1, 1, GRP), lambda g: (g, 0, 0)),
            pl.BlockSpec((F, F), full),
        ],
        out_specs=[
            pl.BlockSpec((SPAN, F), part),
            pl.BlockSpec((2, 32, F), lambda g: (g, 0, 0)),
            pl.BlockSpec((2, 32, F), lambda g: (g, 0, 0)),
            pl.BlockSpec((PLANE, F), full),
            pl.BlockSpec((PLANE, F), full),
        ],
        out_shape=[
            jax.ShapeDtypeStruct((NGRP * SPAN, F), bf16),
            jax.ShapeDtypeStruct((2 * NGRP, 32, F), bf16),
            jax.ShapeDtypeStruct((2 * NGRP, 32, F), bf16),
            jax.ShapeDtypeStruct((PLANE, F), bf16),
            jax.ShapeDtypeStruct((PLANE, F), bf16),
        ],
        compiler_params=pltpu.CompilerParams(dimension_semantics=("arbitrary",)),
        name="encode",
    )(state, feat, cell3, w_enc)


def edge_kernel(feat, pairs, dest, w_pair, w_edge, edge_sum, target, before, taken):
    g = pl.program_id(0)

    @pl.when(g == 0)
    def _():
        i = lax.broadcasted_iota(jnp.int32, (GRP, GRP), 0)
        j = lax.broadcasted_iota(jnp.int32, (GRP, GRP), 1)
        before[...] = jnp.where(i < j, 1.0, 0.0).astype(bf16)
        taken[...] = jnp.zeros((8, F), f32)

    proj = jnp.transpose(dot(feat[...], w_pair[...]).astype(bf16).astype(f32)).astype(bf16)
    send = jnp.concatenate([proj[:F, :HALF], proj[:F, HALF:]], axis=0)
    recv = jnp.concatenate([proj[F:, :HALF], proj[F:, HALF:]], axis=0)
    total = jnp.zeros((HALF, 2 * F), f32)
    for at in range(0, EDGES, ECHUNK):
        s = pairs[0:1, pl.ds(at, ECHUNK)]
        r = pairs[1:2, pl.ds(at, ECHUNK)]
        hot_s = one_hot(HALF, s & (HALF - 1))
        hot_r = one_hot(HALF, r & (HALF - 1))
        up_s = (s & HALF) > 0
        up_r = (r & HALF) > 0
        from_s = dot(send, hot_s)
        from_r = dot(recv, hot_r)
        act = silu(
            jnp.where(up_s, from_s[F:], from_s[:F]) + jnp.where(up_r, from_r[F:], from_r[:F])
        )
        spread = jnp.concatenate(
            [jnp.where(up_r, 0.0, act).astype(bf16), jnp.where(up_r, act, 0.0).astype(bf16)], axis=0
        )
        total = total + dot_nt(hot_r, spread)
    summed = jnp.concatenate([total[:, :F], total[:, F:]], axis=0)
    high = summed.astype(bf16)
    low = (summed - high.astype(f32)).astype(bf16)
    edge_sum[...] = (dot(high, w_edge[...]) + dot(low, w_edge[...])).astype(bf16)

    way = dest[0]
    ways = lax.broadcasted_iota(jnp.int32, (8, GRP), 0)
    mine = jnp.where(ways + 1 == way, 1.0, 0.0)
    earlier = dot(mine.astype(bf16), before[...]) + taken[:, 0:1]
    slot = jnp.sum(mine * (earlier + (ways * CAP).astype(f32)), axis=0, keepdims=True)
    target[0] = jnp.where(way > 0, slot, -1.0).astype(jnp.int32)
    taken[...] = taken[...] + jnp.sum(mine, axis=1, keepdims=True)


def edges(feat, pairs, dest3, w_pair, w_edge):
    full = lambda g: (0, 0)
    part = lambda g: (g, 0)
    row = lambda g: (g, 0, 0)
    return pl.pallas_call(
        edge_kernel,
        grid=(NGRP,),
        in_specs=[
            pl.BlockSpec((GRP, F), part),
            pl.BlockSpec((2, EDGES), lambda g: (0, g)),
            pl.BlockSpec((1, 1, GRP), row),
            pl.BlockSpec((F, 2 * F), full),
            pl.BlockSpec((F, F), full),
        ],
        out_specs=[pl.BlockSpec((GRP, F), part), pl.BlockSpec((1, 1, GRP), row)],
        out_shape=[
            jax.ShapeDtypeStruct((NGRP * GRP, F), bf16),
            jax.ShapeDtypeStruct((NGRP, 1, GRP), jnp.int32),
        ],
        scratch_shapes=[pltpu.VMEM((GRP, GRP), bf16), pltpu.VMEM((8, F), f32)],
        compiler_params=pltpu.CompilerParams(dimension_semantics=("arbitrary",)),
        name="edges",
    )(feat, pairs, dest3, w_pair, w_edge)


def node_kernel(
    before,
    here,
    after,
    x_low,
    x_high,
    y_low,
    y_high,
    feat,
    edge_sum,
    cell,
    dest,
    target,
    mass,
    velocity,
    w_mesh,
    w_node,
    w_accel,
    mesh_out,
    stay_feat,
    vel1_out,
    totals,
    *rest,
):
    packed = rest[:8]
    moved, sums = rest[8:]
    g = pl.program_id(0)
    first = g == 0
    final = g == NGRP - 1

    @pl.when(first)
    def _():
        moved[...] = jnp.zeros_like(moved)
        sums[...] = jnp.zeros_like(sums)

    chunk = 256
    z = lax.broadcasted_iota(jnp.int32, (chunk, F), 0) & 31
    for p in range(2):
        base = p * PLANE
        for at in range(0, PLANE, chunk):
            rows = pl.ds(at, chunk)
            mine = here[pl.ds(base + at, chunk), :].astype(f32)
            if p == 0:
                below = jnp.where(first, x_low[rows, :], before[rows, :])
                above = here[pl.ds(PLANE + at, chunk), :]
            else:
                below = here[rows, :]
                above = jnp.where(final, x_high[rows, :], after[rows, :])
            if at == 0:
                left = jnp.concatenate([y_low[p], here[pl.ds(base, chunk - 32), :]], axis=0)
            else:
                left = here[pl.ds(base + at - 32, chunk), :]
            if at + chunk == PLANE:
                right = jnp.concatenate([here[pl.ds(base + at + 32, chunk - 32), :], y_high[p]], axis=0)
            else:
                right = here[pl.ds(base + at + 32, chunk), :]
            down = jnp.where(z == 0, 0.0, pltpu.roll(mine, 1, 0))
            up = jnp.where(z == 31, 0.0, pltpu.roll(mine, chunk - 1, 0))
            sides = (
                (below.astype(f32) + above.astype(f32))
                + (left.astype(f32) + right.astype(f32))
                + (down + up)
            ).astype(bf16)
            mesh_out[pl.ds(base + at, chunk), :] = (mine + silu(dot(sides, w_mesh[...]))).astype(bf16)

    local = cell[0] - g * SPAN
    way = dest[0]
    ways = lax.broadcasted_iota(jnp.int32, (8, GRP), 0)
    row = (local & (PLANE - 1)).astype(f32)
    plane = (local >> 10).astype(f32)
    stays = jnp.where(way == 0, 1.0, 0.0)
    three = jnp.where(ways == 0, row, jnp.where(ways == 1, plane, stays))
    columns = jnp.transpose(three)
    row_at = columns[:, 0:1].astype(jnp.int32)
    upper = columns[:, 1:2]
    stay = columns[:, 2:3]
    both = jnp.concatenate([mesh_out[pl.ds(0, PLANE), :], mesh_out[pl.ds(PLANE, PLANE), :]], axis=1)
    cells = lax.broadcasted_iota(jnp.int32, (GRP, PLANE), 1)
    hot = jnp.where(cells == row_at, 1.0, 0.0).astype(bf16)
    found = dot(hot, both)
    near = jnp.where(upper > 0.5, found[:, F:], found[:, :F]).astype(bf16)
    update = dot(edge_sum[...], w_node[:F, :]) + dot(near, w_node[F:, :])
    h = (feat[...].astype(f32) + silu(update)).astype(bf16)
    stay_feat[...] = jnp.where(stay > 0.5, h.astype(f32), 0.0).astype(bf16)
    vel1 = velocity[...] + dot_nt(w_accel[...], h)
    vel1_out[...] = vel1
    weight = mass[0]
    sums[0:3, :] = sums[0:3, :] + weight * vel1
    sums[3:4, :] = sums[3:4, :] + weight

    extra = jnp.concatenate([vel1, weight, jnp.zeros((F - 4, GRP), f32)], axis=0)
    wide = jnp.concatenate([h, jnp.transpose(extra).astype(bf16)], axis=1)
    to = target[0]
    for k in range(8):
        rows = pl.ds(k * CAP, CAP)
        moved[rows, :] = moved[rows, :] + dot(one_hot(CAP, to - k * CAP), wide)

    @pl.when(final)
    def _():
        totals[...] = jnp.broadcast_to(jnp.sum(sums[...], axis=1, keepdims=True), (8, F))
        for k in range(8):
            rows = pl.ds(k * CAP, CAP)
            packed[k][0:CAP, :] = moved[rows, 0:F].astype(bf16)
            packed[k][CAP:SENT, :] = jnp.transpose(moved[rows, F:])[0 : SENT - CAP].astype(bf16)


def nodes(mesh1, halos, feat, edge_sum, cell3, dest3, target, mass3, velocity, w_mesh, w_node, w_accel):
    full = lambda g: (0, 0)
    part = lambda g: (g, 0)
    row = lambda g: (g, 0, 0)
    x_low, x_high, y_low, y_high = halos
    return pl.pallas_call(
        node_kernel,
        grid=(NGRP,),
        in_specs=[
            pl.BlockSpec((PLANE, F), lambda g: (jnp.maximum(2 * g - 1, 0), 0)),
            pl.BlockSpec((SPAN, F), part),
            pl.BlockSpec((PLANE, F), lambda g: (jnp.minimum(2 * g + 2, 2 * NGRP - 1), 0)),
            pl.BlockSpec((PLANE, F), full),
            pl.BlockSpec((PLANE, F), full),
            pl.BlockSpec((2, 32, F), row),
            pl.BlockSpec((2, 32, F), row),
            pl.BlockSpec((GRP, F), part),
            pl.BlockSpec((GRP, F), part),
            pl.BlockSpec((1, 1, GRP), row),
            pl.BlockSpec((1, 1, GRP), row),
            pl.BlockSpec((1, 1, GRP), row),
            pl.BlockSpec((1, 1, GRP), row),
            pl.BlockSpec((3, GRP), lambda g: (0, g)),
            pl.BlockSpec((F, F), full),
            pl.BlockSpec((2 * F, F), full),
            pl.BlockSpec((3, F), full),
        ],
        out_specs=[
            pl.BlockSpec((SPAN, F), part),
            pl.BlockSpec((GRP, F), part),
            pl.BlockSpec((3, GRP), lambda g: (0, g)),
            pl.BlockSpec((8, F), full),
        ]
        + [pl.BlockSpec((SENT, F), full)] * 8,
        out_shape=[
            jax.ShapeDtypeStruct((NGRP * SPAN, F), bf16),
            jax.ShapeDtypeStruct((NGRP * GRP, F), bf16),
            jax.ShapeDtypeStruct((3, NGRP * GRP), f32),
            jax.ShapeDtypeStruct((8, F), f32),
        ]
        + [jax.ShapeDtypeStruct((SENT, F), bf16)] * 8,
        scratch_shapes=[pltpu.VMEM((8 * CAP, 2 * F), f32), pltpu.VMEM((8, GRP), f32)],
        compiler_params=pltpu.CompilerParams(dimension_semantics=("arbitrary",)),
        name="nodes",
    )(
        mesh1,
        mesh1,
        mesh1,
        x_low,
        x_high,
        y_low,
        y_high,
        feat,
        edge_sum,
        cell3,
        dest3,
        target,
        mass3,
        velocity,
        w_mesh,
        w_node,
        w_accel,
    )


def finish_kernel(*refs):
    got = refs[:8]
    totals, vel1, dest, arrived_feat, arrived_vel, stay_vel = refs[8:]
    drift = totals[0:3, 0:1] / totals[3:4, 0:1]
    stay_vel[...] = jnp.where(dest[...] == 0, vel1[...] - drift, 0.0)
    for k in range(8):
        arrived_feat[pl.ds(k * CAP, CAP), :] = got[k][0:CAP, :]
        extra = got[k][CAP:SENT, :].astype(f32)
        weight = extra[3:4]
        arrived_vel[0:3, pl.ds(k * CAP, CAP)] = jnp.where(weight > 0, extra[0:3] - drift, 0.0)
        arrived_vel[3:4, pl.ds(k * CAP, CAP)] = weight


def finish(got, totals, vel1, dest2):
    return pl.pallas_call(
        finish_kernel,
        out_shape=[
            jax.ShapeDtypeStruct((8 * CAP, F), bf16),
            jax.ShapeDtypeStruct((4, 8 * CAP), f32),
            jax.ShapeDtypeStruct((3, NGRP * GRP), f32),
        ],
        name="finish",
    )(*got, totals, vel1, dest2)


def ring(block, axis, step):
    size = lax.axis_size(axis)
    return lax.ppermute(block, axis, [(i, (i + step) % size) for i in range(size)])


def offset(block, dx, dy):
    nx, ny = lax.axis_size(GX), lax.axis_size(GY)
    route = [
        (i * ny + j, ((i + dx) % nx) * ny + (j + dy) % ny) for i in range(nx) for j in range(ny)
    ]
    return lax.ppermute(block, GX_GY, route)


def shards(
    mesh_state,
    part_feat,
    cell_index,
    pairs,
    dest,
    mass,
    velocity,
    w_enc,
    w_mesh,
    w_pair,
    w_edge,
    w_node,
    w_accel,
):
    shape = mesh_state.shape
    cell3 = cell_index.reshape(NGRP, 1, GRP)
    dest3 = dest.reshape(NGRP, 1, GRP)
    mass3 = mass.reshape(NGRP, 1, GRP)
    mesh1, y_first, y_last, x_first, x_last = encode(
        mesh_state.reshape(-1, F), part_feat, cell3, w_enc
    )
    halos = (ring(x_last, GX, 1), ring(x_first, GX, -1), ring(y_last, GY, 1), ring(y_first, GY, -1))
    edge_sum, target = edges(part_feat, pairs, dest3, w_pair, w_edge)
    mesh_out, stay_feat, vel1, totals, *packed = nodes(
        mesh1, halos, part_feat, edge_sum, cell3, dest3, target, mass3, velocity, w_mesh, w_node, w_accel
    )
    got = [offset(packed[k], dx, dy) for k, (dx, dy) in enumerate(DIRECTIONS)]
    totals = lax.psum(totals, GX_GY)
    arrived_feat, arrived_vel, stay_vel = finish(got, totals, vel1, dest.reshape(1, -1))
    return (mesh_out.reshape(shape), stay_feat, stay_vel, arrived_feat, arrived_vel)


def solution(mesh):
    torus = Mesh(mesh.devices.reshape(2, 4, 2, 4, 2), ("gx_0", "gx_1", "gx_2", "gy_0", "gy_1"))
    placed = (
        P(GX, GY, None, None),
        P(GX_GY, None),
        P(GX_GY),
        P(None, GX_GY),
        P(GX_GY),
        P(GX_GY),
        P(None, GX_GY),
        P(),
        P(),
        P(),
        P(),
        P(),
        P(),
    )
    return jax.shard_map(
        shards,
        mesh=torus,
        in_specs=placed,
        out_specs=(
            P(GX, GY, None, None),
            P(GX_GY, None),
            P(None, GX_GY),
            P(GX_GY, None),
            P(None, GX_GY),
        ),
        check_vma=False,
    )
```

time: 297 us -> 154 us (0.52)
  matrix products: 148 us -> 0 us
  Pallas kernels: 0 us -> 62.8 us
  blocking collectives: 35.2 us -> 67.1 us
  other arithmetic: 26.6 us -> 0 us
  local copies, waits for them, and re-layouts: 27 us -> 1.4 us
  waiting for transfers between devices: 17.8 us -> 0.03 us
  loops' own time: 16.1 us -> 0 us
    dot_general x68 -> x0, matrix products: 148 us -> none  [the longest x8 32.5 us: particle_one_group(): lax.dot_general(recv_hot.astype(jnp.float32), message, (((0,), (0,)), (()...]
    pallas_call x0 -> x4, Pallas kernels: none -> 62.8 us  [the longest x1 24.7 us: edges(): pl.pallas_call(edge_kernel, grid=(NGRP,), in_specs=[pl.BlockSpec((GRP, F)...]
    psum x5 -> x1, blocking collectives: 35.2 us -> 67.1 us  [shards(): totals = lax.psum(totals, GX_GY)]
    ppermute x12, waiting for transfers between devices: 17.8 us -> 0.03 us  [the longest x8 0.02 us: offset(): return lax.ppermute(block, GX_GY, route)]
    another operation x2 -> x0, loops' own time: 16.1 us -> none  [the longest x1 10.8 us: particle_step(): lax.scan(particle_one_group, 0, (proj_g, feat_g, pair_g, cell_g, rows_g,...]
    dynamic_slice x16 -> x0, local copies, waits for them, and re-layouts: 13.9 us -> none  [encode(): lax.map(encode_one_group, (feat_g, cell_g, numbers)).reshape(-1, width)]
    sub x24 -> x0, other arithmetic: 11.6 us -> none  [the longest x8 6.75 us: particle_one_group(): pair_part[0] - base]
    slice x11 -> x0, local copies, waits for them, and re-layouts: 6.27 us -> none  [the longest x1 4.39 us: shards(): centre = wide[1:-1, 1:-1]]
  transfers between devices with their start and end apart: 12 -> 12, of which waited for: 6 -> 0; matrix products, arithmetic and copies ran while one was open for 3% -> 0% of each run, Pallas kernels for 0% -> 16%
where the time goes in v1:
time: 154 us; the launch traced here: 153 us
  blocking collectives  67.1 us (44%)
  Pallas kernels  62.8 us (41%)
  starting transfers between devices  21.4 us (14%)
    psum x1, blocking collectives, shards(): totals = lax.psum(totals, GX_GY)  67.1 us
    pallas_call x1, Pallas kernels, edges(): pl.pallas_call(edge_kernel, grid=(NGRP,), in_specs=[pl.BlockSpec((GRP, F)...  24.7 us
    pallas_call x1, Pallas kernels, nodes(): pl.pallas_call(node_kernel, grid=(NGRP,), in_specs=[pl.BlockSpec((PLANE,...  22.7 us
    pallas_call x1, Pallas kernels, encode(): pl.pallas_call(encode_kernel, grid=(NGRP,), in_specs=[pl.BlockSpec((SPAN,...  13.7 us
    ppermute x8, starting transfers between devices, offset(): return lax.ppermute(block, GX_GY, route)  10.9 us
    ppermute x4, starting transfers between devices, ring(): lax.ppermute(block, axis, [(i, (i + step) % size) for i in range(size)])  10.5 us
  transfers between devices with their start and end apart: 12, of which 0 were waited for; matrix products, arithmetic and copies ran while one was open for 0% of the time, Pallas kernels for 16%

profile of v1, /device:TPU:0, one launch (start us, length us, event | category | flops | bytes accessed | tf_op | source)
XLA Modules:
  0.0 153.5 jit_solution(13274478813945690396)
XLA Ops:
  0.6 13.7 %encode.1 = (bf16[16384,128]{1,0:T(8,128)(2,1)}, bf16[16,32,128]{2,1,0:T(8,128)(2,1)}, bf16[16,32,128]{2,1,0:T(8,128)(2,1)}, bf16[1024,128]{1,0:T(8,128)(2,1)}, bf16[1024,128]{1,0:T(8,128)(2,1)}) custom-call(bf16[16384,128]{1,0:T(8,128)(2,1)} %bitcast.6, bf16[4096,128]{1,0:T(8,128)(2,1)} %feat.5, s32[8,1,512]{2,1,0:T(1,128)} %bitcast.10, bf16[128,128]{1,0:T(8,128)(2,1)} %w_enc.1), custom_call_target="tpu_custom_call" | custom-call | tf_op jit(solution)/shard_map/encode/pallas_call | solution.py:81
  14.4 0.1 collective-permute-start
  14.5 6.3 %collective-permute-start.1 = (bf16[1024,128]{1,0:T(8,128)(2,1)}, bf16[1024,128]{1,0:T(8,128)(2,1)S(1)}, u32[]{:S(2)}, u32[]{:S(2)}) collective-permute-start(bf16[1024,128]{1,0:T(8,128)(2,1)} %get-tuple-element.29), channel_id=1, source_target_pairs={{0,120},{8,0},{16,8},{24,16},{32,24},{40,32},{48,40},{56,48},{64,5... | collective-permute-start | bytes 786440 | tf_op jit(solution)/shard_map/ppermute | solution.py:376
  20.7 0.7 collective-permute-start.2
  21.5 3.4 %collective-permute-start.3 = (bf16[16,32,128]{2,1,0:T(8,128)(2,1)}, bf16[16,32,128]{2,1,0:T(8,128)(2,1)S(1)}, u32[]{:S(2)}, u32[]{:S(2)}) collective-permute-start(bf16[16,32,128]{2,1,0:T(8,128)(2,1)} %get-tuple-element.31), channel_id=1, source_target_pairs={{0,7},{1,0},{2,1},{3,2},{4,3},{5,4},{6,5},{7,6},{8,15},{9,8},{10,9... | collective-permute-start | bytes 393224 | tf_op jit(solution)/shard_map/ppermute | solution.py:376
  24.9 24.7 %edges.1 = (bf16[4096,128]{1,0:T(8,128)(2,1)}, s32[8,1,512]{2,1,0:T(1,128)}) custom-call(bf16[4096,128]{1,0:T(8,128)(2,1)} %feat.5, s32[2,24576]{1,0:T(2,128)} %pairs.1, s32[8,1,512]{2,1,0:T(1,128)} %bitcast.7, bf16[128,256]{1,0:T(8,128)(2,1)} %w_pair.1, bf16[128,128]{1,0:T(8,128)(2,1)} %w_edge.1), custom_call_target="tpu_custom_call" | custom-call | tf_op jit(solution)/shard_map/edges/pallas_call | solution.py:157
  49.6 0.0 collective-permute-done.2.y_low
  49.6 0.0 copy-start.1
  49.7 0.6 copy-done.2
  50.2 0.0 copy-done.3
  50.3 0.1 copy-done
  50.4 0.1 copy-done.1
  50.5 22.7 %nodes.1 = (bf16[16384,128]{1,0:T(8,128)(2,1)}, bf16[4096,128]{1,0:T(8,128)(2,1)}, f32[3,4096]{1,0:T(4,128)}, f32[8,128]{1,0:T(8,128)}, bf16[144,128]{1,0:T(8,12...) custom-call(bf16[16384,128]{1,0:T(8,128)(2,1)} %get-tuple-element.27, ...), custom_call_target="tpu_custom_call" | custom-call | tf_op jit(solution)/shard_map/nodes/pallas_call | solution.py:289
  73.1 0.1 collective-permute-start.4
  73.2 3.3 %collective-permute-start.5 = (bf16[144,128]{1,0:T(8,128)(2,1)}, bf16[144,128]{1,0:T(8,128)(2,1)S(1)}, u32[]{:S(2)}, u32[]{:S(2)}) collective-permute-start(bf16[144,128]{1,0:T(8,128)(2,1)} %get-tuple-element.37), channel_id=1, source_target_pairs={{0,120},{1,121},{2,122},{3,123},{4,124},{5,125},{6,126},{7,127},{8... | collective-permute-start | bytes 110600 | tf_op jit(solution)/shard_map/ppermute | solution.py:384
  76.5 2.1 %collective-permute-start.7 = (bf16[144,128]{1,0:T(8,128)(2,1)}, bf16[144,128]{1,0:T(8,128)(2,1)S(1)}, u32[]{:S(2)}, u32[]{:S(2)}) collective-permute-start(bf16[144,128]{1,0:T(8,128)(2,1)} %get-tuple-element.39), channel_id=1, source_target_pairs={{0,7},{1,0},{2,1},{3,2},{4,3},{5,4},{6,5},{7,6},{8,15},{9,8},{10,9... | collective-permute-start | bytes 110600 | tf_op jit(solution)/shard_map/ppermute | solution.py:384
  78.6 5.4 %collective-permute-start.9 = (bf16[144,128]{1,0:T(8,128)(2,1)}, bf16[144,128]{1,0:T(8,128)(2,1)S(1)}, u32[]{:S(2)}, u32[]{:S(2)}) collective-permute-start(bf16[144,128]{1,0:T(8,128)(2,1)} %get-tuple-element.41), channel_id=1, source_target_pairs={{0,15},{1,8},{2,9},{3,10},{4,11},{5,12},{6,13},{7,14},{8,23},{9,16... | collective-permute-start | bytes 110600 | tf_op jit(solution)/shard_map/ppermute | solution.py:384
  84.0 0.1 collective-permute-start.11
  84.1 67.1 %psum.7.refs_8_ = f32[8,128]{1,0:T(8,128)} all-reduce(f32[8,128]{1,0:T(8,128)} %get-tuple-element.44), channel_id=1, replica_groups=mesh['gx_0'=2,'gx_1'=4,'gx_2'=2,'gy_0'=4,'gy_1'=2] {'gx_0','gx_1','gx_2'..., use_global_device_ids=true, to_apply=%region_0.0 | all-reduce | flops 1024 | bytes 8192 | tf_op jit(solution)/shard_map/psum | solution.py:415
  151.2 0.5 copy-done.7
  151.7 0.0 copy-done.8
  151.8 0.0 copy-done.9
  151.8 0.0 copy-done.11
  151.8 1.7 %finish.1 = (bf16[1024,128]{1,0:T(8,128)(2,1)}, f32[4,1024]{1,0:T(4,128)}, f32[3,4096]{1,0:T(4,128)}) custom-call(bf16[144,128]{1,0:T(8,128)(2,1)} %copy-done.4, bf16[144,128]{1,0:T(8,128)(2,1)} %copy-done.5, bf16[144,128]{1,0:T(8,128)(2,1)} %copy-done.6, bf16[144,128]{1,0:T(8,128)(2,1)} %copy-done.7, bf16[144,128]{1,0:T(8,128)(2,1)} %copy-done.8, ...), custom_call_target="tpu_custom_call" | custom-call | tf_op jit(solution)/shard_map/finish/pallas_call | solution.py:363
  (29 shorter events, 0.1 us)
Async XLA Ops:
  14.4 35.2 %collective-permute-start = (bf16[1024,128]{1,0:T(8,128)(2,1)}, bf16[1024,128]{1,0:T(8,128)(2,1)S(1)}, u32[]{:S(2)}, u32[]{:S(2)}) collective-permute-start(bf16[1024,128]{1,0:T(8,128)(2,1)} %get-tuple-element.28), channel_id=1, source_target_pairs={{0,8},{8,16},{16,24},{24,32},{32,40},{40,48},{48,56},{56,64},{64,7... | collective-permute-start | bytes 786440 | tf_op jit(solution)/shard_map/ppermute | solution.py:376
  14.5 35.2 %collective-permute-start.1 = (bf16[1024,128]{1,0:T(8,128)(2,1)}, bf16[1024,128]{1,0:T(8,128)(2,1)S(1)}, u32[]{:S(2)}, u32[]{:S(2)}) collective-permute-start(bf16[1024,128]{1,0:T(8,128)(2,1)} %get-tuple-element.29), channel_id=1, source_target_pairs={{0,120},{8,0},{16,8},{24,16},{32,24},{40,32},{48,40},{56,48},{64,5... | collective-permute-start | bytes 786440 | tf_op jit(solution)/shard_map/ppermute | solution.py:376
  20.7 28.8 %collective-permute-start.2 = (bf16[16,32,128]{2,1,0:T(8,128)(2,1)}, bf16[16,32,128]{2,1,0:T(8,128)(2,1)S(1)}, u32[]{:S(2)}, u32[]{:S(2)}) collective-permute-start(bf16[16,32,128]{2,1,0:T(8,128)(2,1)} %get-tuple-element.30), channel_id=1, source_target_pairs={{0,1},{1,2},{2,3},{3,4},{4,5},{5,6},{6,7},{7,0},{8,9},{9,10},{10,1... | collective-permute-start | bytes 393224 | tf_op jit(solution)/shard_map/ppermute | solution.py:376
  21.5 28.1 %collective-permute-start.3 = (bf16[16,32,128]{2,1,0:T(8,128)(2,1)}, bf16[16,32,128]{2,1,0:T(8,128)(2,1)S(1)}, u32[]{:S(2)}, u32[]{:S(2)}) collective-permute-start(bf16[16,32,128]{2,1,0:T(8,128)(2,1)} %get-tuple-element.31), channel_id=1, source_target_pairs={{0,7},{1,0},{2,1},{3,2},{4,3},{5,4},{6,5},{7,6},{8,15},{9,8},{10,9... | collective-permute-start | bytes 393224 | tf_op jit(solution)/shard_map/ppermute | solution.py:376
  49.6 0.7 copy-start.2
  49.6 0.7 copy-start.3
  49.6 0.8 copy-start
  49.6 0.8 copy-start.1
  73.1 5.5 %collective-permute-start.4 = (bf16[144,128]{1,0:T(8,128)(2,1)}, bf16[144,128]{1,0:T(8,128)(2,1)S(1)}, u32[]{:S(2)}, u32[]{:S(2)}) collective-permute-start(bf16[144,128]{1,0:T(8,128)(2,1)} %get-tuple-element.36), channel_id=1, source_target_pairs={{0,127},{1,120},{2,121},{3,122},{4,123},{5,124},{6,125},{7,126},{8... | collective-permute-start | bytes 110600 | tf_op jit(solution)/shard_map/ppermute | solution.py:384
  73.2 10.7 %collective-permute-start.5 = (bf16[144,128]{1,0:T(8,128)(2,1)}, bf16[144,128]{1,0:T(8,128)(2,1)S(1)}, u32[]{:S(2)}, u32[]{:S(2)}) collective-permute-start(bf16[144,128]{1,0:T(8,128)(2,1)} %get-tuple-element.37), channel_id=1, source_target_pairs={{0,120},{1,121},{2,122},{3,123},{4,124},{5,125},{6,126},{7,127},{8... | collective-permute-start | bytes 110600 | tf_op jit(solution)/shard_map/ppermute | solution.py:384
  76.5 7.5 %collective-permute-start.6 = (bf16[144,128]{1,0:T(8,128)(2,1)}, bf16[144,128]{1,0:T(8,128)(2,1)S(1)}, u32[]{:S(2)}, u32[]{:S(2)}) collective-permute-start(bf16[144,128]{1,0:T(8,128)(2,1)} %get-tuple-element.38), channel_id=1, source_target_pairs={{0,121},{1,122},{2,123},{3,124},{4,125},{5,126},{6,127},{7,120},{8... | collective-permute-start | bytes 110600 | tf_op jit(solution)/shard_map/ppermute | solution.py:384
  76.5 74.6 %collective-permute-start.7 = (bf16[144,128]{1,0:T(8,128)(2,1)}, bf16[144,128]{1,0:T(8,128)(2,1)S(1)}, u32[]{:S(2)}, u32[]{:S(2)}) collective-permute-start(bf16[144,128]{1,0:T(8,128)(2,1)} %get-tuple-element.39), channel_id=1, source_target_pairs={{0,7},{1,0},{2,1},{3,2},{4,3},{5,4},{6,5},{7,6},{8,15},{9,8},{10,9... | collective-permute-start | bytes 110600 | tf_op jit(solution)/shard_map/ppermute | solution.py:384
  78.6 72.5 %collective-permute-start.8 = (bf16[144,128]{1,0:T(8,128)(2,1)}, bf16[144,128]{1,0:T(8,128)(2,1)S(1)}, u32[]{:S(2)}, u32[]{:S(2)}) collective-permute-start(bf16[144,128]{1,0:T(8,128)(2,1)} %get-tuple-element.40), channel_id=1, source_target_pairs={{0,1},{1,2},{2,3},{3,4},{4,5},{5,6},{6,7},{7,0},{8,9},{9,10},{10,1... | collective-permute-start | bytes 110600 | tf_op jit(solution)/shard_map/ppermute | solution.py:384
  78.6 72.6 %copy-start.4 = (bf16[144,128]{1,0:T(8,128)(2,1)}, bf16[144,128]{1,0:T(8,128)(2,1)S(1)}, u32[]{:S(2)}) copy-start(bf16[144,128]{1,0:T(8,128)(2,1)S(1)} %collective-permute-done.4.refs_0_) | copy-start | bytes 110596
  78.6 72.6 %collective-permute-start.9 = (bf16[144,128]{1,0:T(8,128)(2,1)}, bf16[144,128]{1,0:T(8,128)(2,1)S(1)}, u32[]{:S(2)}, u32[]{:S(2)}) collective-permute-start(bf16[144,128]{1,0:T(8,128)(2,1)} %get-tuple-element.41), channel_id=1, source_target_pairs={{0,15},{1,8},{2,9},{3,10},{4,11},{5,12},{6,13},{7,14},{8,23},{9,16... | collective-permute-start | bytes 110600 | tf_op jit(solution)/shard_map/ppermute | solution.py:384
  84.0 67.3 %copy-start.5 = (bf16[144,128]{1,0:T(8,128)(2,1)}, bf16[144,128]{1,0:T(8,128)(2,1)S(1)}, u32[]{:S(2)}) copy-start(bf16[144,128]{1,0:T(8,128)(2,1)S(1)} %collective-permute-done.5.refs_1_) | copy-start | bytes 110596
  84.0 67.2 %collective-permute-start.10 = (bf16[144,128]{1,0:T(8,128)(2,1)}, bf16[144,128]{1,0:T(8,128)(2,1)S(1)}, u32[]{:S(2)}, u32[]{:S(2)}) collective-permute-start(bf16[144,128]{1,0:T(8,128)(2,1)} %get-tuple-element.42), channel_id=1, source_target_pairs={{0,8},{1,9},{2,10},{3,11},{4,12},{5,13},{6,14},{7,15},{8,16},{9,17... | collective-permute-start | bytes 110600 | tf_op jit(solution)/shard_map/ppermute | solution.py:384
  84.0 67.3 %copy-start.6 = (bf16[144,128]{1,0:T(8,128)(2,1)}, bf16[144,128]{1,0:T(8,128)(2,1)S(1)}, u32[]{:S(2)}) copy-start(bf16[144,128]{1,0:T(8,128)(2,1)S(1)} %collective-permute-done.6.refs_2_) | copy-start | bytes 110596
  84.0 67.2 %collective-permute-start.11 = (bf16[144,128]{1,0:T(8,128)(2,1)}, bf16[144,128]{1,0:T(8,128)(2,1)S(1)}, u32[]{:S(2)}, u32[]{:S(2)}) collective-permute-start(bf16[144,128]{1,0:T(8,128)(2,1)} %get-tuple-element.43), channel_id=1, source_target_pairs={{0,9},{1,10},{2,11},{3,12},{4,13},{5,14},{6,15},{7,8},{8,17},{9,18... | collective-permute-start | bytes 110600 | tf_op jit(solution)/shard_map/ppermute | solution.py:384
  151.1 0.6 copy-start.7
  151.1 0.6 copy-start.8
  151.2 0.6 copy-start.9
  151.2 0.6 copy-start.10
  151.2 0.6 copy-start.11

commit v2 on v1

--- a/solution.py
+++ b/solution.py
@@ -384,6 +384,13 @@
     return lax.ppermute(block, GX_GY, route)
 
 
+def summed(totals):
+    devices = lax.axis_size(GX_GY)
+    copies = jnp.broadcast_to(totals[0:4, 0], (devices, 1, 4))
+    everyone = lax.all_to_all(copies, GX_GY, 0, 0).reshape(devices, 4)
+    return jnp.broadcast_to(jnp.sum(everyone, axis=0)[:, None], (4, F))
+
+
 def shards(
     mesh_state,
     part_feat,
@@ -412,7 +419,7 @@
         mesh1, halos, part_feat, edge_sum, cell3, dest3, target, mass3, velocity, w_mesh, w_node, w_accel
     )
     got = [offset(packed[k], dx, dy) for k, (dx, dy) in enumerate(DIRECTIONS)]
-    totals = lax.psum(totals, GX_GY)
+    totals = summed(totals)
     arrived_feat, arrived_vel, stay_vel = finish(got, totals, vel1, dest.reshape(1, -1))
     return (mesh_out.reshape(shape), stay_feat, stay_vel, arrived_feat, arrived_vel)
 

time: 154 us -> 107 us (0.69)
  blocking collectives: 67.1 us -> 19.1 us
    psum x1 -> x0, blocking collectives: 67.1 us -> none  [shards(): totals = lax.psum(totals, GX_GY)]
    all_to_all x0 -> x1, blocking collectives: none -> 19.1 us  [summed(): everyone = lax.all_to_all(copies, GX_GY, 0, 0).reshape(devices, 4)]
  transfers between devices with their start and end apart: 12 -> 12, of which waited for: 0 -> 0; matrix products, arithmetic and copies ran while one was open for 0% -> 1% of each run, Pallas kernels for 16% -> 23%
where the time goes in v2:
time: 107 us
  Pallas kernels  62.8 us (59%)
  starting transfers between devices  21.4 us (20%)
  blocking collectives  19.1 us (18%)
  local copies, waits for them, and re-layouts  2.34 us (2%)
    pallas_call x1, Pallas kernels, edges(): pl.pallas_call(edge_kernel, grid=(NGRP,), in_specs=[pl.BlockSpec((GRP, F)...  24.7 us
    pallas_call x1, Pallas kernels, nodes(): pl.pallas_call(node_kernel, grid=(NGRP,), in_specs=[pl.BlockSpec((PLANE,...  22.7 us
    all_to_all x1, blocking collectives, summed(): everyone = lax.all_to_all(copies, GX_GY, 0, 0).reshape(devices, 4)  19.1 us
    pallas_call x1, Pallas kernels, encode(): pl.pallas_call(encode_kernel, grid=(NGRP,), in_specs=[pl.BlockSpec((SPAN,...  13.7 us
    ppermute x8, starting transfers between devices, offset(): return lax.ppermute(block, GX_GY, route)  10.9 us
    ppermute x4, starting transfers between devices, ring(): lax.ppermute(block, axis, [(i, (i + step) % size) for i in range(size)])  10.5 us
  transfers between devices with their start and end apart: 12, of which 0 were waited for; matrix products, arithmetic and copies ran while one was open for 1% of the time, Pallas kernels for 23%

profile of v2, /device:TPU:0, one launch (start us, length us, event | category | flops | bytes accessed | tf_op | source)
XLA Modules:
  0.0 106.7 jit_solution(16976355938524588953)
XLA Ops:
  0.6 13.7 %encode.1 = (bf16[16384,128]{1,0:T(8,128)(2,1)}, bf16[16,32,128]{2,1,0:T(8,128)(2,1)}, bf16[16,32,128]{2,1,0:T(8,128)(2,1)}, bf16[1024,128]{1,0:T(8,128)(2,1)}, bf16[1024,128]{1,0:T(8,128)(2,1)}) custom-call(bf16[16384,128]{1,0:T(8,128)(2,1)} %bitcast.6, bf16[4096,128]{1,0:T(8,128)(2,1)} %feat.5, s32[8,1,512]{2,1,0:T(1,128)} %bitcast.10, bf16[128,128]{1,0:T(8,128)(2,1)} %w_enc.1), custom_call_target="tpu_custom_call" | custom-call | tf_op jit(solution)/shard_map/encode/pallas_call | solution.py:81
  14.4 0.1 collective-permute-start
  14.5 6.3 %collective-permute-start.1 = (bf16[1024,128]{1,0:T(8,128)(2,1)}, bf16[1024,128]{1,0:T(8,128)(2,1)S(1)}, u32[]{:S(2)}, u32[]{:S(2)}) collective-permute-start(bf16[1024,128]{1,0:T(8,128)(2,1)} %get-tuple-element.29), channel_id=1, source_target_pairs={{0,120},{8,0},{16,8},{24,16},{32,24},{40,32},{48,40},{56,48},{64,5... | collective-permute-start | bytes 786440 | tf_op jit(solution)/shard_map/ppermute | solution.py:376
  20.7 0.7 collective-permute-start.2
  21.5 3.4 %collective-permute-start.3 = (bf16[16,32,128]{2,1,0:T(8,128)(2,1)}, bf16[16,32,128]{2,1,0:T(8,128)(2,1)S(1)}, u32[]{:S(2)}, u32[]{:S(2)}) collective-permute-start(bf16[16,32,128]{2,1,0:T(8,128)(2,1)} %get-tuple-element.31), channel_id=1, source_target_pairs={{0,7},{1,0},{2,1},{3,2},{4,3},{5,4},{6,5},{7,6},{8,15},{9,8},{10,9... | collective-permute-start | bytes 393224 | tf_op jit(solution)/shard_map/ppermute | solution.py:376
  24.9 24.7 %edges.1 = (bf16[4096,128]{1,0:T(8,128)(2,1)}, s32[8,1,512]{2,1,0:T(1,128)}) custom-call(bf16[4096,128]{1,0:T(8,128)(2,1)} %feat.5, s32[2,24576]{1,0:T(2,128)} %pairs.1, s32[8,1,512]{2,1,0:T(1,128)} %bitcast.7, bf16[128,256]{1,0:T(8,128)(2,1)} %w_pair.1, bf16[128,128]{1,0:T(8,128)(2,1)} %w_edge.1), custom_call_target="tpu_custom_call" | custom-call | tf_op jit(solution)/shard_map/edges/pallas_call | solution.py:157
  49.6 0.0 collective-permute-done.2.y_low
  49.6 0.0 collective-permute-done.x_low
  49.6 0.0 copy-start.1
  49.7 0.6 copy-done.2
  50.2 0.0 copy-done.3
  50.3 0.1 copy-done
  50.4 0.1 copy-done.1
  50.5 22.7 %nodes.1 = (bf16[16384,128]{1,0:T(8,128)(2,1)}, bf16[4096,128]{1,0:T(8,128)(2,1)}, f32[3,4096]{1,0:T(4,128)}, f32[8,128]{1,0:T(8,128)}, bf16[144,128]{1,0:T(8,12...) custom-call(bf16[16384,128]{1,0:T(8,128)(2,1)} %get-tuple-element.27, ...), custom_call_target="tpu_custom_call" | custom-call | tf_op jit(solution)/shard_map/nodes/pallas_call | solution.py:289
  73.1 0.1 collective-permute-start.4
  73.2 3.3 %collective-permute-start.5 = (bf16[144,128]{1,0:T(8,128)(2,1)}, bf16[144,128]{1,0:T(8,128)(2,1)S(1)}, u32[]{:S(2)}, u32[]{:S(2)}) collective-permute-start(bf16[144,128]{1,0:T(8,128)(2,1)} %get-tuple-element.37), channel_id=1, source_target_pairs={{0,120},{1,121},{2,122},{3,123},{4,124},{5,125},{6,126},{7,127},{8... | collective-permute-start | bytes 110600 | tf_op jit(solution)/shard_map/ppermute | solution.py:384
  76.5 2.1 %collective-permute-start.7 = (bf16[144,128]{1,0:T(8,128)(2,1)}, bf16[144,128]{1,0:T(8,128)(2,1)S(1)}, u32[]{:S(2)}, u32[]{:S(2)}) collective-permute-start(bf16[144,128]{1,0:T(8,128)(2,1)} %get-tuple-element.39), channel_id=1, source_target_pairs={{0,7},{1,0},{2,1},{3,2},{4,3},{5,4},{6,5},{7,6},{8,15},{9,8},{10,9... | collective-permute-start | bytes 110600 | tf_op jit(solution)/shard_map/ppermute | solution.py:384
  78.6 5.4 %collective-permute-start.9 = (bf16[144,128]{1,0:T(8,128)(2,1)}, bf16[144,128]{1,0:T(8,128)(2,1)S(1)}, u32[]{:S(2)}, u32[]{:S(2)}) collective-permute-start(bf16[144,128]{1,0:T(8,128)(2,1)} %get-tuple-element.41), channel_id=1, source_target_pairs={{0,15},{1,8},{2,9},{3,10},{4,11},{5,12},{6,13},{7,14},{8,23},{9,16... | collective-permute-start | bytes 110600 | tf_op jit(solution)/shard_map/ppermute | solution.py:384
  84.0 0.1 collective-permute-start.11
  84.1 0.8 slice_reduce_fusion
  84.9 19.1 %all_to_all.5 = f32[128,1,4]{2,1,0:T(1,128)S(1)} all-to-all(f32[128,1,4]{2,1,0:T(1,128)S(1)} %broadcast_in_dim.4), channel_id=1, replica_groups=mesh['gx_0'=2,'gx_1'=4,'gx_2'=2,'gy_0'=4,'gy_1'=2] {'gx_0','gx_1','gx_2'..., dimensions={0} | all-to-all | bytes 4096 | tf_op jit(solution)/shard_map/all_to_all | solution.py:390
  104.1 0.2 reduce_sum.9
  104.3 0.7 broadcast_in_dim.10.refs_8_
  105.0 1.7 %finish.1 = (bf16[1024,128]{1,0:T(8,128)(2,1)}, f32[4,1024]{1,0:T(4,128)}, f32[3,4096]{1,0:T(4,128)}) custom-call(bf16[144,128]{1,0:T(8,128)(2,1)} %copy-done.4, bf16[144,128]{1,0:T(8,128)(2,1)} %copy-done.5, bf16[144,128]{1,0:T(8,128)(2,1)} %copy-done.6, bf16[144,128]{1,0:T(8,128)(2,1)} %copy-done.7, bf16[144,128]{1,0:T(8,128)(2,1)} %copy-done.8, ...), custom_call_target="tpu_custom_call" | custom-call | tf_op jit(solution)/shard_map/finish/pallas_call | solution.py:363
  (33 shorter events, 0.1 us)
Async XLA Ops:
  14.4 35.2 %collective-permute-start = (bf16[1024,128]{1,0:T(8,128)(2,1)}, bf16[1024,128]{1,0:T(8,128)(2,1)S(1)}, u32[]{:S(2)}, u32[]{:S(2)}) collective-permute-start(bf16[1024,128]{1,0:T(8,128)(2,1)} %get-tuple-element.28), channel_id=1, source_target_pairs={{0,8},{8,16},{16,24},{24,32},{32,40},{40,48},{48,56},{56,64},{64,7... | collective-permute-start | bytes 786440 | tf_op jit(solution)/shard_map/ppermute | solution.py:376
  14.5 35.2 %collective-permute-start.1 = (bf16[1024,128]{1,0:T(8,128)(2,1)}, bf16[1024,128]{1,0:T(8,128)(2,1)S(1)}, u32[]{:S(2)}, u32[]{:S(2)}) collective-permute-start(bf16[1024,128]{1,0:T(8,128)(2,1)} %get-tuple-element.29), channel_id=1, source_target_pairs={{0,120},{8,0},{16,8},{24,16},{32,24},{40,32},{48,40},{56,48},{64,5... | collective-permute-start | bytes 786440 | tf_op jit(solution)/shard_map/ppermute | solution.py:376
  20.7 28.8 %collective-permute-start.2 = (bf16[16,32,128]{2,1,0:T(8,128)(2,1)}, bf16[16,32,128]{2,1,0:T(8,128)(2,1)S(1)}, u32[]{:S(2)}, u32[]{:S(2)}) collective-permute-start(bf16[16,32,128]{2,1,0:T(8,128)(2,1)} %get-tuple-element.30), channel_id=1, source_target_pairs={{0,1},{1,2},{2,3},{3,4},{4,5},{5,6},{6,7},{7,0},{8,9},{9,10},{10,1... | collective-permute-start | bytes 393224 | tf_op jit(solution)/shard_map/ppermute | solution.py:376
  21.5 28.1 %collective-permute-start.3 = (bf16[16,32,128]{2,1,0:T(8,128)(2,1)}, bf16[16,32,128]{2,1,0:T(8,128)(2,1)S(1)}, u32[]{:S(2)}, u32[]{:S(2)}) collective-permute-start(bf16[16,32,128]{2,1,0:T(8,128)(2,1)} %get-tuple-element.31), channel_id=1, source_target_pairs={{0,7},{1,0},{2,1},{3,2},{4,3},{5,4},{6,5},{7,6},{8,15},{9,8},{10,9... | collective-permute-start | bytes 393224 | tf_op jit(solution)/shard_map/ppermute | solution.py:376
  49.6 0.7 copy-start.2
  49.6 0.7 copy-start.3
  49.6 0.8 copy-start
  49.6 0.8 copy-start.1
  73.1 5.5 %collective-permute-start.4 = (bf16[144,128]{1,0:T(8,128)(2,1)}, bf16[144,128]{1,0:T(8,128)(2,1)S(1)}, u32[]{:S(2)}, u32[]{:S(2)}) collective-permute-start(bf16[144,128]{1,0:T(8,128)(2,1)} %get-tuple-element.36), channel_id=1, source_target_pairs={{0,127},{1,120},{2,121},{3,122},{4,123},{5,124},{6,125},{7,126},{8... | collective-permute-start | bytes 110600 | tf_op jit(solution)/shard_map/ppermute | solution.py:384
  73.2 10.7 %collective-permute-start.5 = (bf16[144,128]{1,0:T(8,128)(2,1)}, bf16[144,128]{1,0:T(8,128)(2,1)S(1)}, u32[]{:S(2)}, u32[]{:S(2)}) collective-permute-start(bf16[144,128]{1,0:T(8,128)(2,1)} %get-tuple-element.37), channel_id=1, source_target_pairs={{0,120},{1,121},{2,122},{3,123},{4,124},{5,125},{6,126},{7,127},{8... | collective-permute-start | bytes 110600 | tf_op jit(solution)/shard_map/ppermute | solution.py:384
  76.5 7.5 %collective-permute-start.6 = (bf16[144,128]{1,0:T(8,128)(2,1)}, bf16[144,128]{1,0:T(8,128)(2,1)S(1)}, u32[]{:S(2)}, u32[]{:S(2)}) collective-permute-start(bf16[144,128]{1,0:T(8,128)(2,1)} %get-tuple-element.38), channel_id=1, source_target_pairs={{0,121},{1,122},{2,123},{3,124},{4,125},{5,126},{6,127},{7,120},{8... | collective-permute-start | bytes 110600 | tf_op jit(solution)/shard_map/ppermute | solution.py:384
  76.5 27.7 %collective-permute-start.7 = (bf16[144,128]{1,0:T(8,128)(2,1)}, bf16[144,128]{1,0:T(8,128)(2,1)S(1)}, u32[]{:S(2)}, u32[]{:S(2)}) collective-permute-start(bf16[144,128]{1,0:T(8,128)(2,1)} %get-tuple-element.39), channel_id=1, source_target_pairs={{0,7},{1,0},{2,1},{3,2},{4,3},{5,4},{6,5},{7,6},{8,15},{9,8},{10,9... | collective-permute-start | bytes 110600 | tf_op jit(solution)/shard_map/ppermute | solution.py:384
  78.6 25.6 %collective-permute-start.8 = (bf16[144,128]{1,0:T(8,128)(2,1)}, bf16[144,128]{1,0:T(8,128)(2,1)S(1)}, u32[]{:S(2)}, u32[]{:S(2)}) collective-permute-start(bf16[144,128]{1,0:T(8,128)(2,1)} %get-tuple-element.40), channel_id=1, source_target_pairs={{0,1},{1,2},{2,3},{3,4},{4,5},{5,6},{6,7},{7,0},{8,9},{9,10},{10,1... | collective-permute-start | bytes 110600 | tf_op jit(solution)/shard_map/ppermute | solution.py:384
  78.6 26.4 %copy-start.4 = (bf16[144,128]{1,0:T(8,128)(2,1)}, bf16[144,128]{1,0:T(8,128)(2,1)S(1)}, u32[]{:S(2)}) copy-start(bf16[144,128]{1,0:T(8,128)(2,1)S(1)} %collective-permute-done.4.refs_0_) | copy-start | bytes 110596
  78.6 25.6 %collective-permute-start.9 = (bf16[144,128]{1,0:T(8,128)(2,1)}, bf16[144,128]{1,0:T(8,128)(2,1)S(1)}, u32[]{:S(2)}, u32[]{:S(2)}) collective-permute-start(bf16[144,128]{1,0:T(8,128)(2,1)} %get-tuple-element.41), channel_id=1, source_target_pairs={{0,15},{1,8},{2,9},{3,10},{4,11},{5,12},{6,13},{7,14},{8,23},{9,16... | collective-permute-start | bytes 110600 | tf_op jit(solution)/shard_map/ppermute | solution.py:384
  84.0 21.0 %copy-start.5 = (bf16[144,128]{1,0:T(8,128)(2,1)}, bf16[144,128]{1,0:T(8,128)(2,1)S(1)}, u32[]{:S(2)}) copy-start(bf16[144,128]{1,0:T(8,128)(2,1)S(1)} %collective-permute-done.5.refs_1_) | copy-start | bytes 110596
  84.0 20.3 %collective-permute-start.10 = (bf16[144,128]{1,0:T(8,128)(2,1)}, bf16[144,128]{1,0:T(8,128)(2,1)S(1)}, u32[]{:S(2)}, u32[]{:S(2)}) collective-permute-start(bf16[144,128]{1,0:T(8,128)(2,1)} %get-tuple-element.42), channel_id=1, source_target_pairs={{0,8},{1,9},{2,10},{3,11},{4,12},{5,13},{6,14},{7,15},{8,16},{9,17... | collective-permute-start | bytes 110600 | tf_op jit(solution)/shard_map/ppermute | solution.py:384
  84.0 21.0 %copy-start.6 = (bf16[144,128]{1,0:T(8,128)(2,1)}, bf16[144,128]{1,0:T(8,128)(2,1)S(1)}, u32[]{:S(2)}) copy-start(bf16[144,128]{1,0:T(8,128)(2,1)S(1)} %collective-permute-done.6.refs_2_) | copy-start | bytes 110596
  84.0 20.3 %collective-permute-start.11 = (bf16[144,128]{1,0:T(8,128)(2,1)}, bf16[144,128]{1,0:T(8,128)(2,1)S(1)}, u32[]{:S(2)}, u32[]{:S(2)}) collective-permute-start(bf16[144,128]{1,0:T(8,128)(2,1)} %get-tuple-element.43), channel_id=1, source_target_pairs={{0,9},{1,10},{2,11},{3,12},{4,13},{5,14},{6,15},{7,8},{8,17},{9,18... | collective-permute-start | bytes 110600 | tf_op jit(solution)/shard_map/ppermute | solution.py:384
  104.2 0.8 copy-start.7
  104.2 0.7 copy-start.8
  104.3 0.7 copy-start.9
  104.3 0.7 copy-start.10
  104.3 0.7 copy-start.11

commit v3 on v1

--- a/solution.py
+++ b/solution.py
@@ -5,6 +5,7 @@
 from jax.experimental.pallas import tpu as pltpu
 from jax.sharding import Mesh
 from jax.sharding import PartitionSpec as P
+
 
 GX_GY = ("gx_0", "gx_1", "gx_2", "gy_0", "gy_1")
 GX = ("gx_0", "gx_1", "gx_2")
@@ -21,7 +22,7 @@
 HALF = 256
 CAP = 128
 SENT = 144
-ECHUNK = 512
+ECHUNK = 1024
 
 bf16 = jnp.bfloat16
 f32 = jnp.float32
@@ -42,26 +43,29 @@
 
 def one_hot(rows, index):
     lanes = index.shape[1]
-    return jnp.where(lax.broadcasted_iota(jnp.int32, (rows, lanes), 0) == index, 1.0, 0.0).astype(bf16)
-
-
-def encode_kernel(state, feat, cell, w_enc, mesh1, y_low, y_high, x_low, x_high):
+    mine = lax.broadcasted_iota(jnp.int16, (rows, lanes), 0) == index.astype(jnp.int16)
+    return jnp.where(mine, jnp.ones((), bf16), jnp.zeros((), bf16))
+
+
+def encode_kernel(state, feat, cell, w_enc, mesh1, y_low, y_high, x_low, x_high, w_both):
     g = pl.program_id(0)
+
+    @pl.when(g == 0)
+    def _():
+        w_both[...] = jnp.zeros_like(w_both)
+        w_both[0:F, 0:F] = w_enc[...]
+        w_both[F:, F:] = w_enc[...]
+
     local = cell[0] - g * SPAN
     row = local & (PLANE - 1)
     plane = (local >> 10).astype(f32)
     upper = jnp.transpose(jnp.broadcast_to(plane, (8, GRP)))[:, 0:1]
     rows = feat[...].astype(f32)
     spread = jnp.concatenate([(rows * (1.0 - upper)).astype(bf16), (rows * upper).astype(bf16)], axis=1)
-    chunk = 256
-    for at in range(0, PLANE, chunk):
-        hot = one_hot(chunk, row - at)
-        deposit = dot(hot, spread).astype(bf16)
-        for p in range(2):
-            here = pl.ds(p * PLANE + at, chunk)
-            mesh1[here, :] = (
-                state[here, :].astype(f32) + dot(deposit[:, p * F : (p + 1) * F], w_enc[...])
-            ).astype(bf16)
+    added = dot(dot(one_hot(PLANE, row), spread).astype(bf16), w_both[...])
+    for p in range(2):
+        here = pl.ds(p * PLANE, PLANE)
+        mesh1[here, :] = (state[here, :].astype(f32) + added[:, p * F : (p + 1) * F]).astype(bf16)
     for p in range(2):
         y_low[p] = mesh1[pl.ds(p * PLANE, 32), :]
         y_high[p] = mesh1[pl.ds(p * PLANE + PLANE - 32, 32), :]
@@ -101,6 +105,7 @@
             jax.ShapeDtypeStruct((PLANE, F), bf16),
             jax.ShapeDtypeStruct((PLANE, F), bf16),
         ],
+        scratch_shapes=[pltpu.VMEM((2 * F, 2 * F), bf16)],
         compiler_params=pltpu.CompilerParams(dimension_semantics=("arbitrary",)),
         name="encode",
     )(state, feat, cell3, w_enc)
@@ -127,15 +132,15 @@
         hot_r = one_hot(HALF, r & (HALF - 1))
         up_s = (s & HALF) > 0
         up_r = (r & HALF) > 0
+        zero = jnp.zeros((), bf16)
         from_s = dot(send, hot_s)
         from_r = dot(recv, hot_r)
         act = silu(
             jnp.where(up_s, from_s[F:], from_s[:F]) + jnp.where(up_r, from_r[F:], from_r[:F])
         )
-        spread = jnp.concatenate(
-            [jnp.where(up_r, 0.0, act).astype(bf16), jnp.where(up_r, act, 0.0).astype(bf16)], axis=0
-        )
-        total = total + dot_nt(hot_r, spread)
+        act = act.astype(bf16)
+        spread = jnp.concatenate([jnp.where(up_r, zero, act), jnp.where(up_r, act, zero)], axis=0)
+        total = total + dot(hot_r, jnp.transpose(spread))
     summed = jnp.concatenate([total[:, :F], total[:, F:]], axis=0)
     high = summed.astype(bf16)
     low = (summed - high.astype(f32)).astype(bf16)
@@ -267,10 +272,7 @@
 
     extra = jnp.concatenate([vel1, weight, jnp.zeros((F - 4, GRP), f32)], axis=0)
     wide = jnp.concatenate([h, jnp.transpose(extra).astype(bf16)], axis=1)
-    to = target[0]
-    for k in range(8):
-        rows = pl.ds(k * CAP, CAP)
-        moved[rows, :] = moved[rows, :] + dot(one_hot(CAP, to - k * CAP), wide)
+    moved[...] = moved[...] + dot(one_hot(8 * CAP, target[0]), wide)
 
     @pl.when(final)
     def _():
@@ -384,6 +386,23 @@
     return lax.ppermute(block, GX_GY, route)
 
 
+def swapped(block, axis, flip):
+    return lax.ppermute(block, axis, [(i, i ^ flip) for i in range(lax.axis_size(axis))])
+
+
+STAGES = (("gx_2", 1), ("gy_1", 1), ("gx_1", 1), ("gy_0", 1), ("gx_1", 2), ("gy_0", 2), ("gx_0", 1))
+
+
+def exchange(packed, totals):
+    got = []
+    for k, (dx, dy) in enumerate(DIRECTIONS):
+        got.append(offset(packed[k], dx, dy))
+    for axis, flip in STAGES:
+        theirs = swapped(totals, axis, flip)
+        totals = totals + theirs
+    return got, totals
+
+
 def shards(
     mesh_state,
     part_feat,
@@ -411,8 +430,7 @@
     mesh_out, stay_feat, vel1, totals, *packed = nodes(
         mesh1, halos, part_feat, edge_sum, cell3, dest3, target, mass3, velocity, w_mesh, w_node, w_accel
     )
-    got = [offset(packed[k], dx, dy) for k, (dx, dy) in enumerate(DIRECTIONS)]
-    totals = lax.psum(totals, GX_GY)
+    got, totals = exchange(packed, totals)
     arrived_feat, arrived_vel, stay_vel = finish(got, totals, vel1, dest.reshape(1, -1))
     return (mesh_out.reshape(shape), stay_feat, stay_vel, arrived_feat, arrived_vel)
 

time: 154 us -> 114 us (0.74)
  blocking collectives: 67.1 us -> 0 us
  waiting for transfers between devices: 0.03 us -> 29.9 us
  Pallas kernels: 62.8 us -> 55.8 us
  starting transfers between devices: 21.4 us -> 24.3 us
    psum x1 -> x0, blocking collectives: 67.1 us -> none  [shards(): totals = lax.psum(totals, GX_GY)]
    ppermute x0 -> x7, waiting for transfers between devices: none -> 21.1 us  [swapped(): lax.ppermute(block, axis, [(i, i ^ flip) for i in range(lax.axis_size(axi...]
    ppermute x8, waiting for transfers between devices: 0.02 us -> 8.76 us  [offset(): return lax.ppermute(block, GX_GY, route)]
    pallas_call x1, Pallas kernels: 24.7 us -> 20.4 us  [edges(): pl.pallas_call(edge_kernel, grid=(NGRP,), in_specs=[pl.BlockSpec((GRP, F)...]
    ppermute x0 -> x7, starting transfers between devices: none -> 3.93 us  [swapped(): lax.ppermute(block, axis, [(i, i ^ flip) for i in range(lax.axis_size(axi...]
    pallas_call x1, Pallas kernels: 13.7 us -> 11 us  [encode(): pl.pallas_call(encode_kernel, grid=(NGRP,), in_specs=[pl.BlockSpec((SPAN,...]
  transfers between devices with their start and end apart: 12 -> 19, of which waited for: 0 -> 11; matrix products, arithmetic and copies ran while one was open for 0% -> 1% of each run, Pallas kernels for 16% -> 18%
where the time goes in v3:
time: 114 us
  Pallas kernels  55.8 us (49%)
  waiting for transfers between devices  29.9 us (26%)
  starting transfers between devices  24.3 us (21%)
  local copies, waits for them, and re-layouts  1.4 us (1%)
  other arithmetic  1.29 us (1%)
    pallas_call x1, Pallas kernels, nodes(): pl.pallas_call(node_kernel, grid=(NGRP,), in_specs=[pl.BlockSpec((PLANE,...  22.7 us
    ppermute x7, waiting for transfers between devices, swapped(): lax.ppermute(block, axis, [(i, i ^ flip) for i in range(lax.axis_size(axi...  21.1 us
    pallas_call x1, Pallas kernels, edges(): pl.pallas_call(edge_kernel, grid=(NGRP,), in_specs=[pl.BlockSpec((GRP, F)...  20.4 us
    pallas_call x1, Pallas kernels, encode(): pl.pallas_call(encode_kernel, grid=(NGRP,), in_specs=[pl.BlockSpec((SPAN,...  11 us
    ppermute x4, starting transfers between devices, ring(): lax.ppermute(block, axis, [(i, (i + step) % size) for i in range(size)])  10.5 us
    ppermute x8, starting transfers between devices, offset(): return lax.ppermute(block, GX_GY, route)  9.9 us
    ppermute x8, waiting for transfers between devices, offset(): return lax.ppermute(block, GX_GY, route)  8.76 us
    ppermute x7, starting transfers between devices, swapped(): lax.ppermute(block, axis, [(i, i ^ flip) for i in range(lax.axis_size(axi...  3.93 us
  transfers between devices with their start and end apart: 19, of which 11 were waited for; matrix products, arithmetic and copies ran while one was open for 1% of the time, Pallas kernels for 18%

profile of v3, /device:TPU:0, one launch (start us, length us, event | category | flops | bytes accessed | tf_op | source)
XLA Modules:
  0.0 113.5 jit_solution(3419653556745839583)
XLA Ops:
  0.6 11.0 %encode.1 = (bf16[16384,128]{1,0:T(8,128)(2,1)}, bf16[16,32,128]{2,1,0:T(8,128)(2,1)}, bf16[16,32,128]{2,1,0:T(8,128)(2,1)}, bf16[1024,128]{1,0:T(8,128)(2,1)}, bf16[1024,128]{1,0:T(8,128)(2,1)}) custom-call(bf16[16384,128]{1,0:T(8,128)(2,1)} %bitcast.6, bf16[4096,128]{1,0:T(8,128)(2,1)} %feat.5, s32[8,1,512]{2,1,0:T(1,128)} %bitcast.10, bf16[128,128]{1,0:T(8,128)(2,1)} %w_enc.1), custom_call_target="tpu_custom_call" | custom-call | tf_op jit(solution)/shard_map/encode/pallas_call | solution.py:85
  11.7 6.3 %collective-permute-start.1 = (bf16[1024,128]{1,0:T(8,128)(2,1)}, bf16[1024,128]{1,0:T(8,128)(2,1)S(1)}, u32[]{:S(2)}, u32[]{:S(2)}) collective-permute-start(bf16[1024,128]{1,0:T(8,128)(2,1)} %get-tuple-element.29), channel_id=1, source_target_pairs={{0,120},{8,0},{16,8},{24,16},{32,24},{40,32},{48,40},{56,48},{64,5... | collective-permute-start | bytes 786440 | tf_op jit(solution)/shard_map/ppermute | solution.py:378
  18.0 0.7 collective-permute-start.2
  18.8 3.4 %collective-permute-start.3 = (bf16[16,32,128]{2,1,0:T(8,128)(2,1)}, bf16[16,32,128]{2,1,0:T(8,128)(2,1)S(1)}, u32[]{:S(2)}, u32[]{:S(2)}) collective-permute-start(bf16[16,32,128]{2,1,0:T(8,128)(2,1)} %get-tuple-element.31), channel_id=1, source_target_pairs={{0,7},{1,0},{2,1},{3,2},{4,3},{5,4},{6,5},{7,6},{8,15},{9,8},{10,9... | collective-permute-start | bytes 393224 | tf_op jit(solution)/shard_map/ppermute | solution.py:378
  22.1 20.4 %edges.1 = (bf16[4096,128]{1,0:T(8,128)(2,1)}, s32[8,1,512]{2,1,0:T(1,128)}) custom-call(bf16[4096,128]{1,0:T(8,128)(2,1)} %feat.5, s32[2,24576]{1,0:T(2,128)} %pairs.1, s32[8,1,512]{2,1,0:T(1,128)} %bitcast.7, bf16[128,256]{1,0:T(8,128)(2,1)} %w_pair.1, bf16[128,128]{1,0:T(8,128)(2,1)} %w_edge.1), custom_call_target="tpu_custom_call" | custom-call | tf_op jit(solution)/shard_map/edges/pallas_call | solution.py:162
  43.4 22.7 %nodes.1 = (bf16[16384,128]{1,0:T(8,128)(2,1)}, bf16[4096,128]{1,0:T(8,128)(2,1)}, f32[3,4096]{1,0:T(4,128)}, f32[8,128]{1,0:T(8,128)}, bf16[144,128]{1,0:T(8,12...) custom-call(bf16[16384,128]{1,0:T(8,128)(2,1)} %get-tuple-element.27, ...), custom_call_target="tpu_custom_call" | custom-call | tf_op jit(solution)/shard_map/nodes/pallas_call | solution.py:291
  66.3 3.3 %collective-permute-start.5 = (bf16[144,128]{1,0:T(8,128)(2,1)}, bf16[144,128]{1,0:T(8,128)(2,1)S(1)}, u32[]{:S(2)}, u32[]{:S(2)}) collective-permute-start(bf16[144,128]{1,0:T(8,128)(2,1)} %get-tuple-element.37), channel_id=1, source_target_pairs={{0,120},{1,121},{2,122},{3,123},{4,124},{5,125},{6,126},{7,127},{8... | collective-permute-start | bytes 110600 | tf_op jit(solution)/shard_map/ppermute | solution.py:386
  69.7 1.2 %collective-permute-done.12 = f32[8,128]{1,0:T(8,128)S(1)} collective-permute-done((f32[8,128]{1,0:T(8,128)}, f32[8,128]{1,0:T(8,128)S(1)}, u32[]{:S(2)}, u32[]{:S(2)}) %collective-permute-start.12) | collective-permute-done | bytes 4128 | tf_op jit(solution)/shard_map/ppermute | solution.py:390
  70.9 0.7 add.21
  72.1 3.2 %collective-permute-done.13 = f32[8,128]{1,0:T(8,128)S(1)} collective-permute-done((f32[8,128]{1,0:T(8,128)S(1)}, f32[8,128]{1,0:T(8,128)S(1)}, u32[]{:S(2)}, u32[]{:S(2)}) %collective-permute-start.13) | collective-permute-done | bytes 4128 | tf_op jit(solution)/shard_map/ppermute | solution.py:390
  75.4 3.5 %collective-permute-done.14 = f32[8,128]{1,0:T(8,128)S(1)} collective-permute-done((f32[8,128]{1,0:T(8,128)S(1)}, f32[8,128]{1,0:T(8,128)S(1)}, u32[]{:S(2)}, u32[]{:S(2)}) %collective-permute-start.14) | collective-permute-done | bytes 4128 | tf_op jit(solution)/shard_map/ppermute | solution.py:390
  78.9 3.6 %collective-permute-done.15 = f32[8,128]{1,0:T(8,128)S(1)} collective-permute-done((f32[8,128]{1,0:T(8,128)S(1)}, f32[8,128]{1,0:T(8,128)S(1)}, u32[]{:S(2)}, u32[]{:S(2)}) %collective-permute-start.15) | collective-permute-done | bytes 4128 | tf_op jit(solution)/shard_map/ppermute | solution.py:390
  82.5 5.1 %collective-permute-done.16 = f32[8,128]{1,0:T(8,128)S(1)} collective-permute-done((f32[8,128]{1,0:T(8,128)S(1)}, f32[8,128]{1,0:T(8,128)S(1)}, u32[]{:S(2)}, u32[]{:S(2)}) %collective-permute-start.16) | collective-permute-done | bytes 4128 | tf_op jit(solution)/shard_map/ppermute | solution.py:390
  87.6 1.8 %collective-permute-start.17 = (f32[8,128]{1,0:T(8,128)S(1)}, f32[8,128]{1,0:T(8,128)S(1)}, u32[]{:S(2)}, u32[]{:S(2)}) collective-permute-start(f32[8,128]{1,0:T(8,128)S(1)} %add.25), channel_id=1, source_target_pairs={{0,4},{2,6},{4,0},{6,2},{1,5},{3,7},{5,1},{7,3},{8,12},{10,14},{12... | collective-permute-start | bytes 12296 | tf_op jit(solution)/shard_map/ppermute | solution.py:390
  89.4 3.3 %collective-permute-done.17 = f32[8,128]{1,0:T(8,128)S(1)} collective-permute-done((f32[8,128]{1,0:T(8,128)S(1)}, f32[8,128]{1,0:T(8,128)S(1)}, u32[]{:S(2)}, u32[]{:S(2)}) %collective-permute-start.17) | collective-permute-done | bytes 4128 | tf_op jit(solution)/shard_map/ppermute | solution.py:390
  92.8 1.3 %collective-permute-start.18 = (f32[8,128]{1,0:T(8,128)S(1)}, f32[8,128]{1,0:T(8,128)S(1)}, u32[]{:S(2)}, u32[]{:S(2)}) collective-permute-start(f32[8,128]{1,0:T(8,128)S(1)} %add.26), channel_id=1, source_target_pairs={{0,64},{64,0},{1,65},{65,1},{2,66},{66,2},{3,67},{67,3},{4,68},{68... | collective-permute-start | bytes 12296 | tf_op jit(solution)/shard_map/ppermute | solution.py:390
  94.0 2.6 %collective-permute-start.7 = (bf16[144,128]{1,0:T(8,128)(2,1)}, bf16[144,128]{1,0:T(8,128)(2,1)S(1)}, u32[]{:S(2)}, u32[]{:S(2)}) collective-permute-start(bf16[144,128]{1,0:T(8,128)(2,1)} %get-tuple-element.39), channel_id=1, source_target_pairs={{0,7},{1,0},{2,1},{3,2},{4,3},{5,4},{6,5},{7,6},{8,15},{9,8},{10,9... | collective-permute-start | bytes 110600 | tf_op jit(solution)/shard_map/ppermute | solution.py:386
  96.6 1.3 %collective-permute-done.18 = f32[8,128]{1,0:T(8,128)S(1)} collective-permute-done((f32[8,128]{1,0:T(8,128)S(1)}, f32[8,128]{1,0:T(8,128)S(1)}, u32[]{:S(2)}, u32[]{:S(2)}) %collective-permute-start.18) | collective-permute-done | bytes 4128 | tf_op jit(solution)/shard_map/ppermute | solution.py:390
  98.3 3.5 %collective-permute-start.10 = (bf16[144,128]{1,0:T(8,128)(2,1)}, bf16[144,128]{1,0:T(8,128)(2,1)S(1)}, u32[]{:S(2)}, u32[]{:S(2)}) collective-permute-start(bf16[144,128]{1,0:T(8,128)(2,1)} %get-tuple-element.42), channel_id=1, source_target_pairs={{0,8},{1,9},{2,10},{3,11},{4,12},{5,13},{6,14},{7,15},{8,16},{9,17... | collective-permute-start | bytes 110600 | tf_op jit(solution)/shard_map/ppermute | solution.py:386
  102.5 1.7 %collective-permute-done.8.refs_4_ = bf16[144,128]{1,0:T(8,128)(2,1)S(1)} collective-permute-done((bf16[144,128]{1,0:T(8,128)(2,1)}, bf16[144,128]{1,0:T(8,128)(2,1)S(1)}, u32[]{:S(2)}, u32[]{:S(2)}) %collective-permute-start.8) | collective-permute-done | bytes 36896 | tf_op jit(solution)/shard_map/ppermute | solution.py:386
  104.2 1.1 collective-permute-done.9.refs_5_
  105.2 2.6 %collective-permute-done.10.refs_6_ = bf16[144,128]{1,0:T(8,128)(2,1)S(1)} collective-permute-done((bf16[144,128]{1,0:T(8,128)(2,1)}, bf16[144,128]{1,0:T(8,128)(2,1)S(1)}, u32[]{:S(2)}, u32[]{:S(2)}) %collective-permute-start.10) | collective-permute-done | bytes 36896 | tf_op jit(solution)/shard_map/ppermute | solution.py:386
  107.8 3.5 %collective-permute-done.11.refs_7_ = bf16[144,128]{1,0:T(8,128)(2,1)S(1)} collective-permute-done((bf16[144,128]{1,0:T(8,128)(2,1)}, bf16[144,128]{1,0:T(8,128)(2,1)S(1)}, u32[]{:S(2)}, u32[]{:S(2)}) %collective-permute-start.11) | collective-permute-done | bytes 36896 | tf_op jit(solution)/shard_map/ppermute | solution.py:386
  111.8 1.7 %finish.1 = (bf16[1024,128]{1,0:T(8,128)(2,1)}, f32[4,1024]{1,0:T(4,128)}, f32[3,4096]{1,0:T(4,128)}) custom-call(bf16[144,128]{1,0:T(8,128)(2,1)} %copy-done.4, bf16[144,128]{1,0:T(8,128)(2,1)} %copy-done.5, bf16[144,128]{1,0:T(8,128)(2,1)} %copy-done.6, bf16[144,128]{1,0:T(8,128)(2,1)} %copy-done.7, bf16[144,128]{1,0:T(8,128)(2,1)} %copy-done.8, ...), custom_call_target="tpu_custom_call" | custom-call | tf_op jit(solution)/shard_map/finish/pallas_call | solution.py:365
  (49 shorter events, 3.5 us)
Async XLA Ops:
  11.6 31.0 %collective-permute-start = (bf16[1024,128]{1,0:T(8,128)(2,1)}, bf16[1024,128]{1,0:T(8,128)(2,1)S(1)}, u32[]{:S(2)}, u32[]{:S(2)}) collective-permute-start(bf16[1024,128]{1,0:T(8,128)(2,1)} %get-tuple-element.28), channel_id=1, source_target_pairs={{0,8},{8,16},{16,24},{24,32},{32,40},{40,48},{48,56},{56,64},{64,7... | collective-permute-start | bytes 786440 | tf_op jit(solution)/shard_map/ppermute | solution.py:378
  11.7 30.9 %collective-permute-start.1 = (bf16[1024,128]{1,0:T(8,128)(2,1)}, bf16[1024,128]{1,0:T(8,128)(2,1)S(1)}, u32[]{:S(2)}, u32[]{:S(2)}) collective-permute-start(bf16[1024,128]{1,0:T(8,128)(2,1)} %get-tuple-element.29), channel_id=1, source_target_pairs={{0,120},{8,0},{16,8},{24,16},{32,24},{40,32},{48,40},{56,48},{64,5... | collective-permute-start | bytes 786440 | tf_op jit(solution)/shard_map/ppermute | solution.py:378
  18.0 24.6 %collective-permute-start.2 = (bf16[16,32,128]{2,1,0:T(8,128)(2,1)}, bf16[16,32,128]{2,1,0:T(8,128)(2,1)S(1)}, u32[]{:S(2)}, u32[]{:S(2)}) collective-permute-start(bf16[16,32,128]{2,1,0:T(8,128)(2,1)} %get-tuple-element.30), channel_id=1, source_target_pairs={{0,1},{1,2},{2,3},{3,4},{4,5},{5,6},{6,7},{7,0},{8,9},{9,10},{10,1... | collective-permute-start | bytes 393224 | tf_op jit(solution)/shard_map/ppermute | solution.py:378
  18.8 23.8 %collective-permute-start.3 = (bf16[16,32,128]{2,1,0:T(8,128)(2,1)}, bf16[16,32,128]{2,1,0:T(8,128)(2,1)S(1)}, u32[]{:S(2)}, u32[]{:S(2)}) collective-permute-start(bf16[16,32,128]{2,1,0:T(8,128)(2,1)} %get-tuple-element.31), channel_id=1, source_target_pairs={{0,7},{1,0},{2,1},{3,2},{4,3},{5,4},{6,5},{7,6},{8,15},{9,8},{10,9... | collective-permute-start | bytes 393224 | tf_op jit(solution)/shard_map/ppermute | solution.py:378
  66.2 32.1 %collective-permute-start.4 = (bf16[144,128]{1,0:T(8,128)(2,1)}, bf16[144,128]{1,0:T(8,128)(2,1)S(1)}, u32[]{:S(2)}, u32[]{:S(2)}) collective-permute-start(bf16[144,128]{1,0:T(8,128)(2,1)} %get-tuple-element.36), channel_id=1, source_target_pairs={{0,127},{1,120},{2,121},{3,122},{4,123},{5,124},{6,125},{7,126},{8... | collective-permute-start | bytes 110600 | tf_op jit(solution)/shard_map/ppermute | solution.py:386
  66.3 32.0 %collective-permute-start.5 = (bf16[144,128]{1,0:T(8,128)(2,1)}, bf16[144,128]{1,0:T(8,128)(2,1)S(1)}, u32[]{:S(2)}, u32[]{:S(2)}) collective-permute-start(bf16[144,128]{1,0:T(8,128)(2,1)} %get-tuple-element.37), channel_id=1, source_target_pairs={{0,120},{1,121},{2,122},{3,123},{4,124},{5,125},{6,126},{7,127},{8... | collective-permute-start | bytes 110600 | tf_op jit(solution)/shard_map/ppermute | solution.py:386
  69.6 32.3 %collective-permute-start.6 = (bf16[144,128]{1,0:T(8,128)(2,1)}, bf16[144,128]{1,0:T(8,128)(2,1)S(1)}, u32[]{:S(2)}, u32[]{:S(2)}) collective-permute-start(bf16[144,128]{1,0:T(8,128)(2,1)} %get-tuple-element.38), channel_id=1, source_target_pairs={{0,121},{1,122},{2,123},{3,124},{4,125},{5,126},{6,127},{7,120},{8... | collective-permute-start | bytes 110600 | tf_op jit(solution)/shard_map/ppermute | solution.py:386
  69.6 1.4 %collective-permute-start.12 = (f32[8,128]{1,0:T(8,128)}, f32[8,128]{1,0:T(8,128)S(1)}, u32[]{:S(2)}, u32[]{:S(2)}) collective-permute-start(f32[8,128]{1,0:T(8,128)} %get-tuple-element.44), channel_id=1, source_target_pairs={{0,8},{8,0},{1,9},{9,1},{2,10},{10,2},{3,11},{11,3},{4,12},{12,4},... | collective-permute-start | bytes 12296 | tf_op jit(solution)/shard_map/ppermute | solution.py:390
  71.6 3.7 %collective-permute-start.13 = (f32[8,128]{1,0:T(8,128)S(1)}, f32[8,128]{1,0:T(8,128)S(1)}, u32[]{:S(2)}, u32[]{:S(2)}) collective-permute-start(f32[8,128]{1,0:T(8,128)S(1)} %add.21), channel_id=1, source_target_pairs={{0,1},{1,0},{2,3},{3,2},{4,5},{5,4},{6,7},{7,6},{8,9},{9,8},{10,11... | collective-permute-start | bytes 12296 | tf_op jit(solution)/shard_map/ppermute | solution.py:390
  75.3 3.6 %collective-permute-start.14 = (f32[8,128]{1,0:T(8,128)S(1)}, f32[8,128]{1,0:T(8,128)S(1)}, u32[]{:S(2)}, u32[]{:S(2)}) collective-permute-start(f32[8,128]{1,0:T(8,128)S(1)} %add.22), channel_id=1, source_target_pairs={{0,16},{16,0},{32,48},{48,32},{1,17},{17,1},{33,49},{49,33},{2,18}... | collective-permute-start | bytes 12296 | tf_op jit(solution)/shard_map/ppermute | solution.py:390
  78.9 3.6 %collective-permute-start.15 = (f32[8,128]{1,0:T(8,128)S(1)}, f32[8,128]{1,0:T(8,128)S(1)}, u32[]{:S(2)}, u32[]{:S(2)}) collective-permute-start(f32[8,128]{1,0:T(8,128)S(1)} %add.23), channel_id=1, source_target_pairs={{0,2},{2,0},{4,6},{6,4},{1,3},{3,1},{5,7},{7,5},{8,10},{10,8},{12,... | collective-permute-start | bytes 12296 | tf_op jit(solution)/shard_map/ppermute | solution.py:390
  82.5 5.1 %collective-permute-start.16 = (f32[8,128]{1,0:T(8,128)S(1)}, f32[8,128]{1,0:T(8,128)S(1)}, u32[]{:S(2)}, u32[]{:S(2)}) collective-permute-start(f32[8,128]{1,0:T(8,128)S(1)} %add.24), channel_id=1, source_target_pairs={{0,32},{16,48},{32,0},{48,16},{1,33},{17,49},{33,1},{49,17},{2,34}... | collective-permute-start | bytes 12296 | tf_op jit(solution)/shard_map/ppermute | solution.py:390
  87.6 5.1 %collective-permute-start.17 = (f32[8,128]{1,0:T(8,128)S(1)}, f32[8,128]{1,0:T(8,128)S(1)}, u32[]{:S(2)}, u32[]{:S(2)}) collective-permute-start(f32[8,128]{1,0:T(8,128)S(1)} %add.25), channel_id=1, source_target_pairs={{0,4},{2,6},{4,0},{6,2},{1,5},{3,7},{5,1},{7,3},{8,12},{10,14},{12... | collective-permute-start | bytes 12296 | tf_op jit(solution)/shard_map/ppermute | solution.py:390
  92.8 5.1 %collective-permute-start.18 = (f32[8,128]{1,0:T(8,128)S(1)}, f32[8,128]{1,0:T(8,128)S(1)}, u32[]{:S(2)}, u32[]{:S(2)}) collective-permute-start(f32[8,128]{1,0:T(8,128)S(1)} %add.26), channel_id=1, source_target_pairs={{0,64},{64,0},{1,65},{65,1},{2,66},{66,2},{3,67},{67,3},{4,68},{68... | collective-permute-start | bytes 12296 | tf_op jit(solution)/shard_map/ppermute | solution.py:390
  94.0 8.4 %collective-permute-start.7 = (bf16[144,128]{1,0:T(8,128)(2,1)}, bf16[144,128]{1,0:T(8,128)(2,1)S(1)}, u32[]{:S(2)}, u32[]{:S(2)}) collective-permute-start(bf16[144,128]{1,0:T(8,128)(2,1)} %get-tuple-element.39), channel_id=1, source_target_pairs={{0,7},{1,0},{2,1},{3,2},{4,3},{5,4},{6,5},{7,6},{8,15},{9,8},{10,9... | collective-permute-start | bytes 110600 | tf_op jit(solution)/shard_map/ppermute | solution.py:386
  97.9 6.3 %collective-permute-start.8 = (bf16[144,128]{1,0:T(8,128)(2,1)}, bf16[144,128]{1,0:T(8,128)(2,1)S(1)}, u32[]{:S(2)}, u32[]{:S(2)}) collective-permute-start(bf16[144,128]{1,0:T(8,128)(2,1)} %get-tuple-element.40), channel_id=1, source_target_pairs={{0,1},{1,2},{2,3},{3,4},{4,5},{5,6},{6,7},{7,0},{8,9},{9,10},{10,1... | collective-permute-start | bytes 110600 | tf_op jit(solution)/shard_map/ppermute | solution.py:386
  98.3 12.9 %copy-start.4 = (bf16[144,128]{1,0:T(8,128)(2,1)}, bf16[144,128]{1,0:T(8,128)(2,1)S(1)}, u32[]{:S(2)}) copy-start(bf16[144,128]{1,0:T(8,128)(2,1)S(1)} %collective-permute-done.4.refs_0_) | copy-start | bytes 110596
  98.3 6.9 %collective-permute-start.9 = (bf16[144,128]{1,0:T(8,128)(2,1)}, bf16[144,128]{1,0:T(8,128)(2,1)S(1)}, u32[]{:S(2)}, u32[]{:S(2)}) collective-permute-start(bf16[144,128]{1,0:T(8,128)(2,1)} %get-tuple-element.41), channel_id=1, source_target_pairs={{0,15},{1,8},{2,9},{3,10},{4,11},{5,12},{6,13},{7,14},{8,23},{9,16... | collective-permute-start | bytes 110600 | tf_op jit(solution)/shard_map/ppermute | solution.py:386
  98.3 12.9 %copy-start.5 = (bf16[144,128]{1,0:T(8,128)(2,1)}, bf16[144,128]{1,0:T(8,128)(2,1)S(1)}, u32[]{:S(2)}) copy-start(bf16[144,128]{1,0:T(8,128)(2,1)S(1)} %collective-permute-done.5.refs_1_) | copy-start | bytes 110596
  98.3 9.4 %collective-permute-start.10 = (bf16[144,128]{1,0:T(8,128)(2,1)}, bf16[144,128]{1,0:T(8,128)(2,1)S(1)}, u32[]{:S(2)}, u32[]{:S(2)}) collective-permute-start(bf16[144,128]{1,0:T(8,128)(2,1)} %get-tuple-element.42), channel_id=1, source_target_pairs={{0,8},{1,9},{2,10},{3,11},{4,12},{5,13},{6,14},{7,15},{8,16},{9,17... | collective-permute-start | bytes 110600 | tf_op jit(solution)/shard_map/ppermute | solution.py:386
  101.9 9.4 %copy-start.6 = (bf16[144,128]{1,0:T(8,128)(2,1)}, bf16[144,128]{1,0:T(8,128)(2,1)S(1)}, u32[]{:S(2)}) copy-start(bf16[144,128]{1,0:T(8,128)(2,1)S(1)} %collective-permute-done.6.refs_2_) | copy-start | bytes 110596
  101.9 9.4 %collective-permute-start.11 = (bf16[144,128]{1,0:T(8,128)(2,1)}, bf16[144,128]{1,0:T(8,128)(2,1)S(1)}, u32[]{:S(2)}, u32[]{:S(2)}) collective-permute-start(bf16[144,128]{1,0:T(8,128)(2,1)} %get-tuple-element.43), channel_id=1, source_target_pairs={{0,9},{1,10},{2,11},{3,12},{4,13},{5,14},{6,15},{7,8},{8,17},{9,18... | collective-permute-start | bytes 110600 | tf_op jit(solution)/shard_map/ppermute | solution.py:386
  102.5 8.8 %copy-start.7 = (bf16[144,128]{1,0:T(8,128)(2,1)}, bf16[144,128]{1,0:T(8,128)(2,1)S(1)}, u32[]{:S(2)}) copy-start(bf16[144,128]{1,0:T(8,128)(2,1)S(1)} %collective-permute-done.7.refs_3_) | copy-start | bytes 110596
  104.2 7.1 %copy-start.8 = (bf16[144,128]{1,0:T(8,128)(2,1)}, bf16[144,128]{1,0:T(8,128)(2,1)S(1)}, u32[]{:S(2)}) copy-start(bf16[144,128]{1,0:T(8,128)(2,1)S(1)} %collective-permute-done.8.refs_4_) | copy-start | bytes 110596
  (7 other events, 13.1 us)

commit v4 on v3

--- a/solution.py
+++ b/solution.py
@@ -6,12 +6,12 @@
 from jax.sharding import Mesh
 from jax.sharding import PartitionSpec as P
 
-
 GX_GY = ("gx_0", "gx_1", "gx_2", "gy_0", "gy_1")
 GX = ("gx_0", "gx_1", "gx_2")
 GY = ("gy_0", "gy_1")
 
-DIRECTIONS = ((-1, -1), (-1, 0), (-1, 1), (0, -1), (0, 1), (1, -1), (1, 0), (1, 1))
+PLACES = ((0, 0), (0, 1), (0, 2), (2, 0), (3, 0), (1, 0), (1, 1), (1, 2))
+PARTS = (3, 3, 1, 1)
 
 F = 128
 GRP = 512
@@ -47,22 +47,15 @@
     return jnp.where(mine, jnp.ones((), bf16), jnp.zeros((), bf16))
 
 
-def encode_kernel(state, feat, cell, w_enc, mesh1, y_low, y_high, x_low, x_high, w_both):
+def encode_kernel(state, feat, cell, w_enc, mesh1, y_low, y_high, x_low, x_high):
     g = pl.program_id(0)
-
-    @pl.when(g == 0)
-    def _():
-        w_both[...] = jnp.zeros_like(w_both)
-        w_both[0:F, 0:F] = w_enc[...]
-        w_both[F:, F:] = w_enc[...]
-
     local = cell[0] - g * SPAN
     row = local & (PLANE - 1)
     plane = (local >> 10).astype(f32)
     upper = jnp.transpose(jnp.broadcast_to(plane, (8, GRP)))[:, 0:1]
-    rows = feat[...].astype(f32)
+    rows = dot(feat[...], w_enc[...])
     spread = jnp.concatenate([(rows * (1.0 - upper)).astype(bf16), (rows * upper).astype(bf16)], axis=1)
-    added = dot(dot(one_hot(PLANE, row), spread).astype(bf16), w_both[...])
+    added = dot(one_hot(PLANE, row), spread)
     for p in range(2):
         here = pl.ds(p * PLANE, PLANE)
         mesh1[here, :] = (state[here, :].astype(f32) + added[:, p * F : (p + 1) * F]).astype(bf16)
@@ -105,7 +98,6 @@
             jax.ShapeDtypeStruct((PLANE, F), bf16),
             jax.ShapeDtypeStruct((PLANE, F), bf16),
         ],
-        scratch_shapes=[pltpu.VMEM((2 * F, 2 * F), bf16)],
         compiler_params=pltpu.CompilerParams(dimension_semantics=("arbitrary",)),
         name="encode",
     )(state, feat, cell3, w_enc)
@@ -204,8 +196,8 @@
     totals,
     *rest,
 ):
-    packed = rest[:8]
-    moved, sums = rest[8:]
+    packed = rest[:4]
+    moved, riding, sums = rest[4:]
     g = pl.program_id(0)
     first = g == 0
     final = g == NGRP - 1
@@ -213,6 +205,7 @@
     @pl.when(first)
     def _():
         moved[...] = jnp.zeros_like(moved)
+        riding[...] = jnp.zeros_like(riding)
         sums[...] = jnp.zeros_like(sums)
 
     chunk = 256
@@ -251,7 +244,7 @@
     row = (local & (PLANE - 1)).astype(f32)
     plane = (local >> 10).astype(f32)
     stays = jnp.where(way == 0, 1.0, 0.0)
-    three = jnp.where(ways == 0, row, jnp.where(ways == 1, plane, stays))
+    three = jnp.where(ways == 0, row, jnp.where(ways == 1, plane, jnp.where(ways == 2, stays, way.astype(f32))))
     columns = jnp.transpose(three)
     row_at = columns[:, 0:1].astype(jnp.int32)
     upper = columns[:, 1:2]
@@ -270,17 +263,33 @@
     sums[0:3, :] = sums[0:3, :] + weight * vel1
     sums[3:4, :] = sums[3:4, :] + weight
 
-    extra = jnp.concatenate([vel1, weight, jnp.zeros((F - 4, GRP), f32)], axis=0)
-    wide = jnp.concatenate([h, jnp.transpose(extra).astype(bf16)], axis=1)
-    moved[...] = moved[...] + dot(one_hot(8 * CAP, target[0]), wide)
+    extra = jnp.concatenate([vel1, weight, jnp.zeros((12, GRP), f32)], axis=0)
+    extras = jnp.concatenate([jnp.where(way == k + 1, extra, 0.0) for k in range(8)], axis=0)
+    extras = jnp.transpose(extras).astype(bf16)
+    goes = columns[:, 3:4]
+    full = h.astype(f32)
+    halves = jnp.concatenate(
+        [
+            jnp.where((goes > 0.5) & (goes < 4.5), full, 0.0).astype(bf16),
+            jnp.where(goes > 4.5, full, 0.0).astype(bf16),
+        ],
+        axis=1,
+    )
+    to = target[0]
+    moved[...] = moved[...] + dot(one_hot(4 * CAP, to & (4 * CAP - 1)), halves)
+    riding[...] = riding[...] + dot(one_hot(CAP, to & (CAP - 1)), extras)
 
     @pl.when(final)
     def _():
-        totals[...] = jnp.broadcast_to(jnp.sum(sums[...], axis=1, keepdims=True), (8, F))
+        column = jnp.broadcast_to(jnp.sum(sums[...], axis=1, keepdims=True), (8, F))
+        totals[...] = jnp.broadcast_to(jnp.transpose(column)[0:1, 0:4], (F, 4))[:, None, :]
+        rode = jnp.transpose(riding[...]).astype(bf16)
         for k in range(8):
-            rows = pl.ds(k * CAP, CAP)
-            packed[k][0:CAP, :] = moved[rows, 0:F].astype(bf16)
-            packed[k][CAP:SENT, :] = jnp.transpose(moved[rows, F:])[0 : SENT - CAP].astype(bf16)
+            rows = pl.ds(k % 4 * CAP, CAP)
+            lanes = pl.ds(k // 4 * F, F)
+            to, place = PLACES[k]
+            packed[to][pl.ds(place * SENT, CAP), :] = moved[rows, lanes].astype(bf16)
+            packed[to][pl.ds(place * SENT + CAP, SENT - CAP), :] = rode[k * 16 : (k + 1) * 16]
 
 
 def nodes(mesh1, halos, feat, edge_sum, cell3, dest3, target, mass3, velocity, w_mesh, w_node, w_accel):
@@ -314,17 +323,17 @@
             pl.BlockSpec((SPAN, F), part),
             pl.BlockSpec((GRP, F), part),
             pl.BlockSpec((3, GRP), lambda g: (0, g)),
-            pl.BlockSpec((8, F), full),
+            pl.BlockSpec((F, 1, 4), lambda g: (0, 0, 0)),
         ]
-        + [pl.BlockSpec((SENT, F), full)] * 8,
+        + [pl.BlockSpec((n * SENT, F), full) for n in PARTS],
         out_shape=[
             jax.ShapeDtypeStruct((NGRP * SPAN, F), bf16),
             jax.ShapeDtypeStruct((NGRP * GRP, F), bf16),
             jax.ShapeDtypeStruct((3, NGRP * GRP), f32),
-            jax.ShapeDtypeStruct((8, F), f32),
+            jax.ShapeDtypeStruct((F, 1, 4), f32),
         ]
-        + [jax.ShapeDtypeStruct((SENT, F), bf16)] * 8,
-        scratch_shapes=[pltpu.VMEM((8 * CAP, 2 * F), f32), pltpu.VMEM((8, GRP), f32)],
+        + [jax.ShapeDtypeStruct((n * SENT, F), bf16) for n in PARTS],
+        scratch_shapes=[pltpu.VMEM((4 * CAP, 2 * F), f32), pltpu.VMEM((CAP, F), f32), pltpu.VMEM((8, GRP), f32)],
         compiler_params=pltpu.CompilerParams(dimension_semantics=("arbitrary",)),
         name="nodes",
     )(
@@ -348,20 +357,45 @@
     )
 
 
-def finish_kernel(*refs):
-    got = refs[:8]
-    totals, vel1, dest, arrived_feat, arrived_vel, stay_vel = refs[8:]
-    drift = totals[0:3, 0:1] / totals[3:4, 0:1]
+def relay_kernel(from_high, from_low, own_down, own_up, down, up):
+    for ref, own, at in ((down, own_down, 0), (up, own_up, 2)):
+        there = pl.ds(at * SENT, SENT)
+        ref[0:SENT, :] = from_high[there, :]
+        ref[SENT : 2 * SENT, :] = own[...]
+        ref[2 * SENT : 3 * SENT, :] = from_low[there, :]
+
+
+def relay(from_high, from_low, own_down, own_up):
+    return pl.pallas_call(
+        relay_kernel,
+        out_shape=[jax.ShapeDtypeStruct((3 * SENT, F), bf16)] * 2,
+        name="relay",
+    )(from_high, from_low, own_down, own_up)
+
+
+def finish_kernel(from_high, from_low, down, up, totals, vel1, dest, arrived_feat, arrived_vel, stay_vel):
+    total = jnp.transpose(jnp.broadcast_to(jnp.sum(totals[...], axis=0), (8, 4)))
+    drift = total[0:3, 0:1] / total[3:4, 0:1]
     stay_vel[...] = jnp.where(dest[...] == 0, vel1[...] - drift, 0.0)
-    for k in range(8):
-        arrived_feat[pl.ds(k * CAP, CAP), :] = got[k][0:CAP, :]
-        extra = got[k][CAP:SENT, :].astype(f32)
+    sources = (
+        (down, 0),
+        (from_high, 1),
+        (up, 0),
+        (down, 1),
+        (up, 1),
+        (down, 2),
+        (from_low, 1),
+        (up, 2),
+    )
+    for k, (ref, at) in enumerate(sources):
+        arrived_feat[pl.ds(k * CAP, CAP), :] = ref[pl.ds(at * SENT, CAP), :]
+        extra = ref[pl.ds(at * SENT + CAP, SENT - CAP), :].astype(f32)
         weight = extra[3:4]
         arrived_vel[0:3, pl.ds(k * CAP, CAP)] = jnp.where(weight > 0, extra[0:3] - drift, 0.0)
         arrived_vel[3:4, pl.ds(k * CAP, CAP)] = weight
 
 
-def finish(got, totals, vel1, dest2):
+def finish(*args):
     return pl.pallas_call(
         finish_kernel,
         out_shape=[
@@ -370,37 +404,12 @@
             jax.ShapeDtypeStruct((3, NGRP * GRP), f32),
         ],
         name="finish",
-    )(*got, totals, vel1, dest2)
+    )(*args)
 
 
 def ring(block, axis, step):
     size = lax.axis_size(axis)
     return lax.ppermute(block, axis, [(i, (i + step) % size) for i in range(size)])
-
-
-def offset(block, dx, dy):
-    nx, ny = lax.axis_size(GX), lax.axis_size(GY)
-    route = [
-        (i * ny + j, ((i + dx) % nx) * ny + (j + dy) % ny) for i in range(nx) for j in range(ny)
-    ]
-    return lax.ppermute(block, GX_GY, route)
-
-
-def swapped(block, axis, flip):
-    return lax.ppermute(block, axis, [(i, i ^ flip) for i in range(lax.axis_size(axis))])
-
-
-STAGES = (("gx_2", 1), ("gy_1", 1), ("gx_1", 1), ("gy_0", 1), ("gx_1", 2), ("gy_0", 2), ("gx_0", 1))
-
-
-def exchange(packed, totals):
-    got = []
-    for k, (dx, dy) in enumerate(DIRECTIONS):
-        got.append(offset(packed[k], dx, dy))
-    for axis, flip in STAGES:
-        theirs = swapped(totals, axis, flip)
-        totals = totals + theirs
-    return got, totals
 
 
 def shards(
@@ -430,8 +439,15 @@
     mesh_out, stay_feat, vel1, totals, *packed = nodes(
         mesh1, halos, part_feat, edge_sum, cell3, dest3, target, mass3, velocity, w_mesh, w_node, w_accel
     )
-    got, totals = exchange(packed, totals)
-    arrived_feat, arrived_vel, stay_vel = finish(got, totals, vel1, dest.reshape(1, -1))
+    to_low, to_high, own_down, own_up = packed
+    from_high, from_low = ring(to_low, GX, -1), ring(to_high, GX, 1)
+    totals = lax.all_to_all(totals, GX_GY, 0, 0)
+    own_down, own_up, totals = lax.optimization_barrier((own_down, own_up, totals))
+    down, up = relay(from_high, from_low, own_down, own_up)
+    down, up = ring(down, GY, -1), ring(up, GY, 1)
+    arrived_feat, arrived_vel, stay_vel = finish(
+        from_high, from_low, down, up, totals, vel1, dest.reshape(1, -1)
+    )
     return (mesh_out.reshape(shape), stay_feat, stay_vel, arrived_feat, arrived_vel)
 
 

time: 114 us -> 95.8 us (0.84)
  waiting for transfers between devices: 29.9 us -> 6.16 us
  blocking collectives: 0 us -> 17.9 us
  starting transfers between devices: 24.3 us -> 13.1 us
  local copies, waits for them, and re-layouts: 1.4 us -> 2.74 us
  Pallas kernels: 55.8 us -> 54.5 us
  other arithmetic: 1.29 us -> 0 us
    ppermute x15 -> x0, waiting for transfers between devices: 29.9 us -> none  [the longest x7 21.1 us: swapped(): lax.ppermute(block, axis, [(i, i ^ flip) for i in range(lax.axis_size(axi...]
    all_to_all x0 -> x1, blocking collectives: none -> 17.9 us  [shards(): totals = lax.all_to_all(totals, GX_GY, 0, 0)]
    ppermute x15 -> x0, starting transfers between devices: 13.8 us -> none  [the longest x8 9.9 us: offset(): return lax.ppermute(block, GX_GY, route)]
    ppermute x4 -> x8, waiting for transfers between devices: 0.01 us -> 6.16 us  [ring(): lax.ppermute(block, axis, [(i, (i + step) % size) for i in range(size)])]
    ppermute x4 -> x8, starting transfers between devices: 10.5 us -> 13.1 us  [ring(): lax.ppermute(block, axis, [(i, (i + step) % size) for i in range(size)])]
    pallas_call x1, Pallas kernels: 22.7 us -> 20.4 us  [nodes(): pl.pallas_call(node_kernel, grid=(NGRP,), in_specs=[pl.BlockSpec((PLANE,...]
    pallas_call x0 -> x1, Pallas kernels: none -> 1.64 us  [relay(): pl.pallas_call(relay_kernel, out_shape=[jax.ShapeDtypeStruct((3 * SENT, F...]
    unnamed x24 -> x16, local copies, waits for them, and re-layouts: 1.4 us -> 2.74 us
  transfers between devices with their start and end apart: 19 -> 8, of which waited for: 11 -> 2; matrix products, arithmetic and copies ran while one was open for 1% -> 0% of each run, Pallas kernels for 18% -> 21%
where the time goes in v4:
time: 95.8 us; the launch traced here: 95.2 us
  Pallas kernels  54.5 us (57%)
  blocking collectives  17.9 us (19%)
  starting transfers between devices  13.1 us (14%)
  waiting for transfers between devices  6.16 us (6%)
  local copies, waits for them, and re-layouts  2.74 us (3%)
    pallas_call x1, Pallas kernels, nodes(): pl.pallas_call(node_kernel, grid=(NGRP,), in_specs=[pl.BlockSpec((PLANE,...  20.4 us
    pallas_call x1, Pallas kernels, edges(): pl.pallas_call(edge_kernel, grid=(NGRP,), in_specs=[pl.BlockSpec((GRP, F)...  20.4 us
    all_to_all x1, blocking collectives, shards(): totals = lax.all_to_all(totals, GX_GY, 0, 0)  17.9 us
    ppermute x8, starting transfers between devices, ring(): lax.ppermute(block, axis, [(i, (i + step) % size) for i in range(size)])  13.1 us
    pallas_call x1, Pallas kernels, encode(): pl.pallas_call(encode_kernel, grid=(NGRP,), in_specs=[pl.BlockSpec((SPAN,...  10 us
    ppermute x8, waiting for transfers between devices, ring(): lax.ppermute(block, axis, [(i, (i + step) % size) for i in range(size)])  6.16 us
    unnamed x16, local copies, waits for them, and re-layouts  2.74 us
    pallas_call x1, Pallas kernels, finish(): pl.pallas_call(finish_kernel, out_shape=[jax.ShapeDtypeStruct((8 * CAP, F...  2.03 us
  transfers between devices with their start and end apart: 8, of which 2 were waited for; matrix products, arithmetic and copies ran while one was open for 0% of the time, Pallas kernels for 21%

profile of v4, /device:TPU:0, one launch (start us, length us, event | category | flops | bytes accessed | tf_op | source)
XLA Modules:
  0.0 95.2 jit_solution(2414482939786991882)
XLA Ops:
  0.6 10.0 %encode.1 = (bf16[16384,128]{1,0:T(8,128)(2,1)}, bf16[16,32,128]{2,1,0:T(8,128)(2,1)}, bf16[16,32,128]{2,1,0:T(8,128)(2,1)}, bf16[1024,128]{1,0:T(8,128)(2,1)}, bf16[1024,128]{1,0:T(8,128)(2,1)}) custom-call(bf16[16384,128]{1,0:T(8,128)(2,1)} %bitcast.6, bf16[4096,128]{1,0:T(8,128)(2,1)} %feat.5, s32[8,1,512]{2,1,0:T(1,128)} %bitcast.10, bf16[128,128]{1,0:T(8,128)(2,1)} %w_enc.1), custom_call_target="tpu_custom_call" | custom-call | tf_op jit(solution)/shard_map/encode/pallas_call | solution.py:78
  10.7 0.1 collective-permute-start
  10.8 6.3 %collective-permute-start.1 = (bf16[1024,128]{1,0:T(8,128)(2,1)}, bf16[1024,128]{1,0:T(8,128)(2,1)S(1)}, u32[]{:S(2)}, u32[]{:S(2)}) collective-permute-start(bf16[1024,128]{1,0:T(8,128)(2,1)} %get-tuple-element.30), channel_id=1, source_target_pairs={{0,120},{8,0},{16,8},{24,16},{32,24},{40,32},{48,40},{56,48},{64,5... | collective-permute-start | bytes 786440 | tf_op jit(solution)/shard_map/ppermute | solution.py:412
  17.0 0.7 collective-permute-start.2
  17.8 3.4 %collective-permute-start.3 = (bf16[16,32,128]{2,1,0:T(8,128)(2,1)}, bf16[16,32,128]{2,1,0:T(8,128)(2,1)S(1)}, u32[]{:S(2)}, u32[]{:S(2)}) collective-permute-start(bf16[16,32,128]{2,1,0:T(8,128)(2,1)} %get-tuple-element.32), channel_id=1, source_target_pairs={{0,7},{1,0},{2,1},{3,2},{4,3},{5,4},{6,5},{7,6},{8,15},{9,8},{10,9... | collective-permute-start | bytes 393224 | tf_op jit(solution)/shard_map/ppermute | solution.py:412
  21.2 20.4 %edges.1 = (bf16[4096,128]{1,0:T(8,128)(2,1)}, s32[8,1,512]{2,1,0:T(1,128)}) custom-call(bf16[4096,128]{1,0:T(8,128)(2,1)} %feat.5, s32[2,24576]{1,0:T(2,128)} %pairs.1, s32[8,1,512]{2,1,0:T(1,128)} %bitcast.7, bf16[128,256]{1,0:T(8,128)(2,1)} %w_pair.1, bf16[128,128]{1,0:T(8,128)(2,1)} %w_edge.1), custom_call_target="tpu_custom_call" | custom-call | tf_op jit(solution)/shard_map/edges/pallas_call | solution.py:154
  41.6 0.0 copy-start.3
  41.7 0.6 copy-done.4
  42.3 0.0 copy-done.5
  42.3 0.1 copy-done.2
  42.4 0.0 copy-done.3
  42.5 20.4 %nodes.1 = (bf16[16384,128]{1,0:T(8,128)(2,1)}, bf16[4096,128]{1,0:T(8,128)(2,1)}, f32[3,4096]{1,0:T(4,128)}, f32[128,1,4]{2,1,0:T(1,128)}, bf16[432,128]{1,0:T(...) custom-call(bf16[16384,128]{1,0:T(8,128)(2,1)} %get-tuple-element.28.before.here.after, ...), custom_call_target="tpu_custom_call" | custom-call | tf_op jit(solution)/shard_map/nodes/pallas_call | solution.py:300
  62.9 0.2 collective-permute-start.4
  63.1 0.4 collective-permute-start.5
  63.5 17.9 %all_to_all.5.totals = f32[128,1,4]{2,1,0:T(1,128)} all-to-all(f32[128,1,4]{2,1,0:T(1,128)} %get-tuple-element.41), channel_id=1, replica_groups=mesh['gx_0'=2,'gx_1'=4,'gx_2'=2,'gy_0'=4,'gy_1'=2] {'gx_0','gx_1','gx_2'..., dimensions={0} | all-to-all | bytes 4096 | tf_op jit(solution)/shard_map/all_to_all | solution.py:444
  81.4 0.6 copy-done
  82.0 0.6 copy-done.1
  82.7 1.6 %relay.1 = (bf16[432,128]{1,0:T(8,128)(2,1)}, bf16[432,128]{1,0:T(8,128)(2,1)}) custom-call(bf16[432,128]{1,0:T(8,128)(2,1)} %copy-done, bf16[432,128]{1,0:T(8,128)(2,1)} %copy-done.1, bf16[144,128]{1,0:T(8,128)(2,1)} %get-tuple-element.42.own_down, bf16[144,128]{1,0:T(8,128)(2,1)} %get-tuple-element.43.own_up), custom_call_target="tpu_custom_call" | custom-call | tf_op jit(solution)/shard_map/relay/pallas_call | solution.py:369
  84.3 0.7 collective-permute-start.6
  85.0 1.4 %collective-permute-start.7 = (bf16[432,128]{1,0:T(8,128)(2,1)}, bf16[432,128]{1,0:T(8,128)(2,1)S(1)}, u32[]{:S(2)}, u32[]{:S(2)}) collective-permute-start(bf16[432,128]{1,0:T(8,128)(2,1)} %get-tuple-element.45), channel_id=1, source_target_pairs={{0,1},{1,2},{2,3},{3,4},{4,5},{5,6},{6,7},{7,0},{8,9},{9,10},{10,1... | collective-permute-start | bytes 331784 | tf_op jit(solution)/shard_map/ppermute | solution.py:412
  86.3 2.9 %collective-permute-done.6.down = bf16[432,128]{1,0:T(8,128)(2,1)S(1)} collective-permute-done((bf16[432,128]{1,0:T(8,128)(2,1)}, bf16[432,128]{1,0:T(8,128)(2,1)S(1)}, u32[]{:S(2)}, u32[]{:S(2)}) %collective-permute-start.6) | collective-permute-done | bytes 110624 | tf_op jit(solution)/shard_map/ppermute | solution.py:412
  89.3 3.2 %collective-permute-done.7.up = bf16[432,128]{1,0:T(8,128)(2,1)S(1)} collective-permute-done((bf16[432,128]{1,0:T(8,128)(2,1)}, bf16[432,128]{1,0:T(8,128)(2,1)S(1)}, u32[]{:S(2)}, u32[]{:S(2)}) %collective-permute-start.7) | collective-permute-done | bytes 110624 | tf_op jit(solution)/shard_map/ppermute | solution.py:412
  92.5 0.6 copy-done.7
  93.1 2.0 %finish.1 = (bf16[1024,128]{1,0:T(8,128)(2,1)}, f32[4,1024]{1,0:T(4,128)}, f32[3,4096]{1,0:T(4,128)}) custom-call(bf16[432,128]{1,0:T(8,128)(2,1)} %copy-done, bf16[432,128]{1,0:T(8,128)(2,1)} %copy-done.1, bf16[432,128]{1,0:T(8,128)(2,1)} %copy-done.6, bf16[432,128]{1,0:T(8,128)(2,1)} %copy-done.7, f32[128,1,4]{2,1,0:T(1,128)} %all_to_all.5.totals, ...), custom_call_target="tpu_custom_call" | custom-call | tf_op jit(solution)/shard_map/finish/pallas_call | solution.py:399
  (14 shorter events, 0.0 us)
Async XLA Ops:
  10.7 31.0 %collective-permute-start = (bf16[1024,128]{1,0:T(8,128)(2,1)}, bf16[1024,128]{1,0:T(8,128)(2,1)S(1)}, u32[]{:S(2)}, u32[]{:S(2)}) collective-permute-start(bf16[1024,128]{1,0:T(8,128)(2,1)} %get-tuple-element.29), channel_id=1, source_target_pairs={{0,8},{8,16},{16,24},{24,32},{32,40},{40,48},{48,56},{56,64},{64,7... | collective-permute-start | bytes 786440 | tf_op jit(solution)/shard_map/ppermute | solution.py:412
  10.8 30.9 %collective-permute-start.1 = (bf16[1024,128]{1,0:T(8,128)(2,1)}, bf16[1024,128]{1,0:T(8,128)(2,1)S(1)}, u32[]{:S(2)}, u32[]{:S(2)}) collective-permute-start(bf16[1024,128]{1,0:T(8,128)(2,1)} %get-tuple-element.30), channel_id=1, source_target_pairs={{0,120},{8,0},{16,8},{24,16},{32,24},{40,32},{48,40},{56,48},{64,5... | collective-permute-start | bytes 786440 | tf_op jit(solution)/shard_map/ppermute | solution.py:412
  17.0 24.6 %collective-permute-start.2 = (bf16[16,32,128]{2,1,0:T(8,128)(2,1)}, bf16[16,32,128]{2,1,0:T(8,128)(2,1)S(1)}, u32[]{:S(2)}, u32[]{:S(2)}) collective-permute-start(bf16[16,32,128]{2,1,0:T(8,128)(2,1)} %get-tuple-element.31), channel_id=1, source_target_pairs={{0,1},{1,2},{2,3},{3,4},{4,5},{5,6},{6,7},{7,0},{8,9},{9,10},{10,1... | collective-permute-start | bytes 393224 | tf_op jit(solution)/shard_map/ppermute | solution.py:412
  17.8 23.8 %collective-permute-start.3 = (bf16[16,32,128]{2,1,0:T(8,128)(2,1)}, bf16[16,32,128]{2,1,0:T(8,128)(2,1)S(1)}, u32[]{:S(2)}, u32[]{:S(2)}) collective-permute-start(bf16[16,32,128]{2,1,0:T(8,128)(2,1)} %get-tuple-element.32), channel_id=1, source_target_pairs={{0,7},{1,0},{2,1},{3,2},{4,3},{5,4},{6,5},{7,6},{8,15},{9,8},{10,9... | collective-permute-start | bytes 393224 | tf_op jit(solution)/shard_map/ppermute | solution.py:412
  41.6 0.7 copy-start.4
  41.6 0.7 copy-start.5
  41.6 0.8 copy-start.2
  41.6 0.8 copy-start.3
  62.9 18.5 %collective-permute-start.4 = (bf16[432,128]{1,0:T(8,128)(2,1)}, bf16[432,128]{1,0:T(8,128)(2,1)S(1)}, u32[]{:S(2)}, u32[]{:S(2)}) collective-permute-start(bf16[432,128]{1,0:T(8,128)(2,1)} %get-tuple-element.37), channel_id=1, source_target_pairs={{0,120},{8,0},{16,8},{24,16},{32,24},{40,32},{48,40},{56,48},{64,5... | collective-permute-start | bytes 331784 | tf_op jit(solution)/shard_map/ppermute | solution.py:412
  63.1 18.3 %collective-permute-start.5 = (bf16[432,128]{1,0:T(8,128)(2,1)}, bf16[432,128]{1,0:T(8,128)(2,1)S(1)}, u32[]{:S(2)}, u32[]{:S(2)}) collective-permute-start(bf16[432,128]{1,0:T(8,128)(2,1)} %get-tuple-element.38), channel_id=1, source_target_pairs={{0,8},{8,16},{16,24},{24,32},{32,40},{40,48},{48,56},{56,64},{64,7... | collective-permute-start | bytes 331784 | tf_op jit(solution)/shard_map/ppermute | solution.py:412
  81.4 0.6 copy-start
  82.0 0.6 copy-start.1
  84.3 5.0 %collective-permute-start.6 = (bf16[432,128]{1,0:T(8,128)(2,1)}, bf16[432,128]{1,0:T(8,128)(2,1)S(1)}, u32[]{:S(2)}, u32[]{:S(2)}) collective-permute-start(bf16[432,128]{1,0:T(8,128)(2,1)} %get-tuple-element.44), channel_id=1, source_target_pairs={{0,7},{1,0},{2,1},{3,2},{4,3},{5,4},{6,5},{7,6},{8,15},{9,8},{10,9... | collective-permute-start | bytes 331784 | tf_op jit(solution)/shard_map/ppermute | solution.py:412
  85.0 7.5 %collective-permute-start.7 = (bf16[432,128]{1,0:T(8,128)(2,1)}, bf16[432,128]{1,0:T(8,128)(2,1)S(1)}, u32[]{:S(2)}, u32[]{:S(2)}) collective-permute-start(bf16[432,128]{1,0:T(8,128)(2,1)} %get-tuple-element.45), channel_id=1, source_target_pairs={{0,1},{1,2},{2,3},{3,4},{4,5},{5,6},{6,7},{7,0},{8,9},{9,10},{10,1... | collective-permute-start | bytes 331784 | tf_op jit(solution)/shard_map/ppermute | solution.py:412
  89.3 3.2 %copy-start.6 = (bf16[432,128]{1,0:T(8,128)(2,1)}, bf16[432,128]{1,0:T(8,128)(2,1)S(1)}, u32[]{:S(2)}) copy-start(bf16[432,128]{1,0:T(8,128)(2,1)S(1)} %collective-permute-done.6.down) | copy-start | bytes 331780
  92.5 0.6 copy-start.7

commit v5 on v4

--- a/solution.py
+++ b/solution.py
@@ -357,6 +357,10 @@
     )
 
 
+def near(block):
+    return pltpu.with_memory_space_constraint(block, pltpu.VMEM)
+
+
 def relay_kernel(from_high, from_low, own_down, own_up, down, up):
     for ref, own, at in ((down, own_down, 0), (up, own_up, 2)):
         there = pl.ds(at * SENT, SENT)
@@ -435,16 +439,19 @@
         mesh_state.reshape(-1, F), part_feat, cell3, w_enc
     )
     halos = (ring(x_last, GX, 1), ring(x_first, GX, -1), ring(y_last, GY, 1), ring(y_first, GY, -1))
+    halos = tuple(near(block) for block in halos)
     edge_sum, target = edges(part_feat, pairs, dest3, w_pair, w_edge)
     mesh_out, stay_feat, vel1, totals, *packed = nodes(
         mesh1, halos, part_feat, edge_sum, cell3, dest3, target, mass3, velocity, w_mesh, w_node, w_accel
     )
     to_low, to_high, own_down, own_up = packed
     from_high, from_low = ring(to_low, GX, -1), ring(to_high, GX, 1)
+    from_high, from_low = near(from_high), near(from_low)
+    down, up = relay(from_high, from_low, own_down, own_up)
+    down, up, totals = lax.optimization_barrier((down, up, totals))
+    down, up = ring(down, GY, -1), ring(up, GY, 1)
     totals = lax.all_to_all(totals, GX_GY, 0, 0)
-    own_down, own_up, totals = lax.optimization_barrier((own_down, own_up, totals))
-    down, up = relay(from_high, from_low, own_down, own_up)
-    down, up = ring(down, GY, -1), ring(up, GY, 1)
+    down, up = near(down), near(up)
     arrived_feat, arrived_vel, stay_vel = finish(
         from_high, from_low, down, up, totals, vel1, dest.reshape(1, -1)
     )

time: 95.8 us -> 91.9 us (0.959)
  local copies, waits for them, and re-layouts: 2.74 us -> 0 us
  blocking collectives: 17.9 us -> 16.2 us
  waiting for transfers between devices: 6.16 us -> 7.62 us
    unnamed x16 -> x0, local copies, waits for them, and re-layouts: 2.74 us -> none
    all_to_all x1, blocking collectives: 17.9 us -> 16.2 us  [shards(): totals = lax.all_to_all(totals, GX_GY, 0, 0)]
    ppermute x8, waiting for transfers between devices: 6.16 us -> 7.62 us  [ring(): lax.ppermute(block, axis, [(i, (i + step) % size) for i in range(size)])]
  transfers between devices with their start and end apart: 8 -> 8, of which waited for: 2 -> 2; matrix products, arithmetic and copies ran while one was open for 0% -> 0% of each run, Pallas kernels for 21% -> 22%
where the time goes in v5:
time: 91.9 us; the launch traced here: 91.3 us
  Pallas kernels  53.8 us (59%)
  blocking collectives  16.2 us (18%)
  starting transfers between devices  13.1 us (14%)
  waiting for transfers between devices  7.62 us (8%)
    pallas_call x1, Pallas kernels, edges(): pl.pallas_call(edge_kernel, grid=(NGRP,), in_specs=[pl.BlockSpec((GRP, F)...  20.4 us
    pallas_call x1, Pallas kernels, nodes(): pl.pallas_call(node_kernel, grid=(NGRP,), in_specs=[pl.BlockSpec((PLANE,...  20 us
    all_to_all x1, blocking collectives, shards(): totals = lax.all_to_all(totals, GX_GY, 0, 0)  16.2 us
    ppermute x8, starting transfers between devices, ring(): lax.ppermute(block, axis, [(i, (i + step) % size) for i in range(size)])  13.1 us
    pallas_call x1, Pallas kernels, encode(): pl.pallas_call(encode_kernel, grid=(NGRP,), in_specs=[pl.BlockSpec((SPAN,...  10 us
    ppermute x8, waiting for transfers between devices, ring(): lax.ppermute(block, axis, [(i, (i + step) % size) for i in range(size)])  7.62 us
  transfers between devices with their start and end apart: 8, of which 2 were waited for; matrix products, arithmetic and copies ran while one was open for 0% of the time, Pallas kernels for 22%

profile of v5, /device:TPU:0, one launch (start us, length us, event | category | flops | bytes accessed | tf_op | source)
XLA Modules:
  0.0 91.3 jit_solution(14628462827715135356)
XLA Ops:
  0.6 10.0 %encode.1 = (bf16[16384,128]{1,0:T(8,128)(2,1)}, bf16[16,32,128]{2,1,0:T(8,128)(2,1)}, bf16[16,32,128]{2,1,0:T(8,128)(2,1)}, bf16[1024,128]{1,0:T(8,128)(2,1)}, bf16[1024,128]{1,0:T(8,128)(2,1)}) custom-call(bf16[16384,128]{1,0:T(8,128)(2,1)} %bitcast.6, bf16[4096,128]{1,0:T(8,128)(2,1)} %feat.5, s32[8,1,512]{2,1,0:T(1,128)} %bitcast.10, bf16[128,128]{1,0:T(8,128)(2,1)} %w_enc.1), custom_call_target="tpu_custom_call" | custom-call | tf_op jit(solution)/shard_map/encode/pallas_call | solution.py:78
  10.7 0.1 collective-permute-start
  10.8 6.3 %collective-permute-start.1 = (bf16[1024,128]{1,0:T(8,128)(2,1)}, bf16[1024,128]{1,0:T(8,128)(2,1)S(1)}, u32[]{:S(2)}, u32[]{:S(2)}) collective-permute-start(bf16[1024,128]{1,0:T(8,128)(2,1)} %get-tuple-element.30), channel_id=1, source_target_pairs={{0,120},{8,0},{16,8},{24,16},{32,24},{40,32},{48,40},{56,48},{64,5... | collective-permute-start | bytes 786440 | tf_op jit(solution)/shard_map/ppermute | solution.py:416
  17.0 0.7 collective-permute-start.2
  17.8 3.4 %collective-permute-start.3 = (bf16[16,32,128]{2,1,0:T(8,128)(2,1)}, bf16[16,32,128]{2,1,0:T(8,128)(2,1)S(1)}, u32[]{:S(2)}, u32[]{:S(2)}) collective-permute-start(bf16[16,32,128]{2,1,0:T(8,128)(2,1)} %get-tuple-element.32), channel_id=1, source_target_pairs={{0,7},{1,0},{2,1},{3,2},{4,3},{5,4},{6,5},{7,6},{8,15},{9,8},{10,9... | collective-permute-start | bytes 393224 | tf_op jit(solution)/shard_map/ppermute | solution.py:416
  21.2 20.4 %edges.1 = (bf16[4096,128]{1,0:T(8,128)(2,1)}, s32[8,1,512]{2,1,0:T(1,128)}) custom-call(bf16[4096,128]{1,0:T(8,128)(2,1)} %feat.5, s32[2,24576]{1,0:T(2,128)} %pairs.1, s32[8,1,512]{2,1,0:T(1,128)} %bitcast.7, bf16[128,256]{1,0:T(8,128)(2,1)} %w_pair.1, bf16[128,128]{1,0:T(8,128)(2,1)} %w_edge.1), custom_call_target="tpu_custom_call" | custom-call | tf_op jit(solution)/shard_map/edges/pallas_call | solution.py:154
  41.6 0.0 collective-permute-done.2.y_low
  41.6 0.0 collective-permute-done.3.y_high
  41.6 0.0 collective-permute-done.x_low
  41.6 0.0 collective-permute-done.1.x_high
  41.6 20.0 %nodes.1 = (bf16[16384,128]{1,0:T(8,128)(2,1)}, bf16[4096,128]{1,0:T(8,128)(2,1)}, f32[3,4096]{1,0:T(4,128)}, f32[128,1,4]{2,1,0:T(1,128)}, bf16[432,128]{1,0:T(...) custom-call(bf16[16384,128]{1,0:T(8,128)(2,1)} %get-tuple-element.28.before.here.after, ...), custom_call_target="tpu_custom_call" | custom-call | tf_op jit(solution)/shard_map/nodes/pallas_call | solution.py:300
  61.7 0.2 collective-permute-start.4
  61.8 0.4 collective-permute-start.5
  62.2 2.3 %collective-permute-done.4.from_high = bf16[432,128]{1,0:T(8,128)(2,1)S(1)} collective-permute-done((bf16[432,128]{1,0:T(8,128)(2,1)}, bf16[432,128]{1,0:T(8,128)(2,1)S(1)}, u32[]{:S(2)}, u32[]{:S(2)}) %collective-permute-start.4) | collective-permute-done | bytes 110624 | tf_op jit(solution)/shard_map/ppermute | solution.py:416
  64.5 5.4 %collective-permute-done.5.from_low = bf16[432,128]{1,0:T(8,128)(2,1)S(1)} collective-permute-done((bf16[432,128]{1,0:T(8,128)(2,1)}, bf16[432,128]{1,0:T(8,128)(2,1)S(1)}, u32[]{:S(2)}, u32[]{:S(2)}) %collective-permute-start.5) | collective-permute-done | bytes 110624 | tf_op jit(solution)/shard_map/ppermute | solution.py:416
  69.8 1.5 %relay.1 = (bf16[432,128]{1,0:T(8,128)(2,1)}, bf16[432,128]{1,0:T(8,128)(2,1)}) custom-call(bf16[432,128]{1,0:T(8,128)(2,1)S(1)} %collective-permute-done.4.from_high, bf16[432,128]{1,0:T(8,128)(2,1)S(1)} %collective-permute-done.5.from_low, bf16[144,128]{1,0:T(8,128)(2,1)} %get-tuple-element.39.own_down, bf16[144,128]{1,0:T(8,128)(2,1)} %get-tuple-element.40.own_up), custom_call_target="tpu_custom_call" | custom-call | tf_op jit(solution)/shard_map/relay/pallas_call | solution.py:373
  71.3 0.8 collective-permute-start.6
  72.1 1.2 %collective-permute-start.7 = (bf16[432,128]{1,0:T(8,128)(2,1)}, bf16[432,128]{1,0:T(8,128)(2,1)S(1)}, u32[]{:S(2)}, u32[]{:S(2)}) collective-permute-start(bf16[432,128]{1,0:T(8,128)(2,1)} %get-tuple-element.45), channel_id=1, source_target_pairs={{0,1},{1,2},{2,3},{3,4},{4,5},{5,6},{6,7},{7,0},{8,9},{9,10},{10,1... | collective-permute-start | bytes 331784 | tf_op jit(solution)/shard_map/ppermute | solution.py:416
  73.3 16.2 %all_to_all.5.totals = f32[128,1,4]{2,1,0:T(1,128)} all-to-all(f32[128,1,4]{2,1,0:T(1,128)} %get-tuple-element.46), channel_id=1, replica_groups=mesh['gx_0'=2,'gx_1'=4,'gx_2'=2,'gy_0'=4,'gy_1'=2] {'gx_0','gx_1','gx_2'..., dimensions={0} | all-to-all | bytes 4096 | tf_op jit(solution)/shard_map/all_to_all | solution.py:453
  89.5 0.0 collective-permute-done.6.down
  89.5 0.0 collective-permute-done.7.up
  89.5 1.8 %finish.1 = (bf16[1024,128]{1,0:T(8,128)(2,1)}, f32[4,1024]{1,0:T(4,128)}, f32[3,4096]{1,0:T(4,128)}) custom-call(bf16[432,128]{1,0:T(8,128)(2,1)S(1)} %collective-permute-done.4.from_high, bf16[432,128]{1,0:T(8,128)(2,1)S(1)} %collective-permute-done.5.from_low, bf16[432,128]{1,0:T(8,128)(2,1)S(1)} %collective-permute-done.6.down, ...), custom_call_target="tpu_custom_call" | custom-call | tf_op jit(solution)/shard_map/finish/pallas_call | solution.py:403
Async XLA Ops:
  10.7 30.9 %collective-permute-start = (bf16[1024,128]{1,0:T(8,128)(2,1)}, bf16[1024,128]{1,0:T(8,128)(2,1)S(1)}, u32[]{:S(2)}, u32[]{:S(2)}) collective-permute-start(bf16[1024,128]{1,0:T(8,128)(2,1)} %get-tuple-element.29), channel_id=1, source_target_pairs={{0,8},{8,16},{16,24},{24,32},{32,40},{40,48},{48,56},{56,64},{64,7... | collective-permute-start | bytes 786440 | tf_op jit(solution)/shard_map/ppermute | solution.py:416
  10.8 30.9 %collective-permute-start.1 = (bf16[1024,128]{1,0:T(8,128)(2,1)}, bf16[1024,128]{1,0:T(8,128)(2,1)S(1)}, u32[]{:S(2)}, u32[]{:S(2)}) collective-permute-start(bf16[1024,128]{1,0:T(8,128)(2,1)} %get-tuple-element.30), channel_id=1, source_target_pairs={{0,120},{8,0},{16,8},{24,16},{32,24},{40,32},{48,40},{56,48},{64,5... | collective-permute-start | bytes 786440 | tf_op jit(solution)/shard_map/ppermute | solution.py:416
  17.0 24.6 %collective-permute-start.2 = (bf16[16,32,128]{2,1,0:T(8,128)(2,1)}, bf16[16,32,128]{2,1,0:T(8,128)(2,1)S(1)}, u32[]{:S(2)}, u32[]{:S(2)}) collective-permute-start(bf16[16,32,128]{2,1,0:T(8,128)(2,1)} %get-tuple-element.31), channel_id=1, source_target_pairs={{0,1},{1,2},{2,3},{3,4},{4,5},{5,6},{6,7},{7,0},{8,9},{9,10},{10,1... | collective-permute-start | bytes 393224 | tf_op jit(solution)/shard_map/ppermute | solution.py:416
  17.8 23.8 %collective-permute-start.3 = (bf16[16,32,128]{2,1,0:T(8,128)(2,1)}, bf16[16,32,128]{2,1,0:T(8,128)(2,1)S(1)}, u32[]{:S(2)}, u32[]{:S(2)}) collective-permute-start(bf16[16,32,128]{2,1,0:T(8,128)(2,1)} %get-tuple-element.32), channel_id=1, source_target_pairs={{0,7},{1,0},{2,1},{3,2},{4,3},{5,4},{6,5},{7,6},{8,15},{9,8},{10,9... | collective-permute-start | bytes 393224 | tf_op jit(solution)/shard_map/ppermute | solution.py:416
  61.7 2.8 %collective-permute-start.4 = (bf16[432,128]{1,0:T(8,128)(2,1)}, bf16[432,128]{1,0:T(8,128)(2,1)S(1)}, u32[]{:S(2)}, u32[]{:S(2)}) collective-permute-start(bf16[432,128]{1,0:T(8,128)(2,1)} %get-tuple-element.37), channel_id=1, source_target_pairs={{0,120},{8,0},{16,8},{24,16},{32,24},{40,32},{48,40},{56,48},{64,5... | collective-permute-start | bytes 331784 | tf_op jit(solution)/shard_map/ppermute | solution.py:416
  61.8 8.0 %collective-permute-start.5 = (bf16[432,128]{1,0:T(8,128)(2,1)}, bf16[432,128]{1,0:T(8,128)(2,1)S(1)}, u32[]{:S(2)}, u32[]{:S(2)}) collective-permute-start(bf16[432,128]{1,0:T(8,128)(2,1)} %get-tuple-element.38), channel_id=1, source_target_pairs={{0,8},{8,16},{16,24},{24,32},{32,40},{40,48},{48,56},{56,64},{64,7... | collective-permute-start | bytes 331784 | tf_op jit(solution)/shard_map/ppermute | solution.py:416
  71.3 18.2 %collective-permute-start.6 = (bf16[432,128]{1,0:T(8,128)(2,1)}, bf16[432,128]{1,0:T(8,128)(2,1)S(1)}, u32[]{:S(2)}, u32[]{:S(2)}) collective-permute-start(bf16[432,128]{1,0:T(8,128)(2,1)} %get-tuple-element.44), channel_id=1, source_target_pairs={{0,7},{1,0},{2,1},{3,2},{4,3},{5,4},{6,5},{7,6},{8,15},{9,8},{10,9... | collective-permute-start | bytes 331784 | tf_op jit(solution)/shard_map/ppermute | solution.py:416
  72.1 17.4 %collective-permute-start.7 = (bf16[432,128]{1,0:T(8,128)(2,1)}, bf16[432,128]{1,0:T(8,128)(2,1)S(1)}, u32[]{:S(2)}, u32[]{:S(2)}) collective-permute-start(bf16[432,128]{1,0:T(8,128)(2,1)} %get-tuple-element.45), channel_id=1, source_target_pairs={{0,1},{1,2},{2,3},{3,4},{4,5},{5,6},{6,7},{7,0},{8,9},{9,10},{10,1... | collective-permute-start | bytes 331784 | tf_op jit(solution)/shard_map/ppermute | solution.py:416

commit v6 on v5

--- a/solution.py
+++ b/solution.py
@@ -23,6 +23,7 @@
 CAP = 128
 SENT = 144
 ECHUNK = 1024
+LOOKED = 256
 
 bf16 = jnp.bfloat16
 f32 = jnp.float32
@@ -45,6 +46,19 @@
     lanes = index.shape[1]
     mine = lax.broadcasted_iota(jnp.int16, (rows, lanes), 0) == index.astype(jnp.int16)
     return jnp.where(mine, jnp.ones((), bf16), jnp.zeros((), bf16))
+
+
+def looked_up(table, index):
+    lane = jnp.broadcast_to(index & (F - 1), (F, F))
+    found = [
+        jnp.take_along_axis(table[:, at : at + F], lane, axis=1, mode="promise_in_bounds")
+        for at in range(0, GRP, F)
+    ]
+    odd = (index & F) > 0
+    upper = (index & HALF) > 0
+    return jnp.where(
+        upper, jnp.where(odd, found[3], found[2]), jnp.where(odd, found[1], found[0])
+    )
 
 
 def encode_kernel(state, feat, cell, w_enc, mesh1, y_low, y_high, x_low, x_high):
@@ -113,22 +127,27 @@
         before[...] = jnp.where(i < j, 1.0, 0.0).astype(bf16)
         taken[...] = jnp.zeros((8, F), f32)
 
-    proj = jnp.transpose(dot(feat[...], w_pair[...]).astype(bf16).astype(f32)).astype(bf16)
-    send = jnp.concatenate([proj[:F, :HALF], proj[:F, HALF:]], axis=0)
-    recv = jnp.concatenate([proj[F:, :HALF], proj[F:, HALF:]], axis=0)
+    proj = jnp.transpose(dot(feat[...], w_pair[...]).astype(bf16).astype(f32))
+    send = proj[:F]
+    send_two = jnp.concatenate([proj[:F, :HALF], proj[:F, HALF:]], axis=0).astype(bf16)
+    recv = jnp.concatenate([proj[F:, :HALF], proj[F:, HALF:]], axis=0).astype(bf16)
     total = jnp.zeros((HALF, 2 * F), f32)
     for at in range(0, EDGES, ECHUNK):
         s = pairs[0:1, pl.ds(at, ECHUNK)]
         r = pairs[1:2, pl.ds(at, ECHUNK)]
-        hot_s = one_hot(HALF, s & (HALF - 1))
         hot_r = one_hot(HALF, r & (HALF - 1))
-        up_s = (s & HALF) > 0
         up_r = (r & HALF) > 0
         zero = jnp.zeros((), bf16)
-        from_s = dot(send, hot_s)
+        rest = s[:, LOOKED:]
+        by_product = dot(send_two, one_hot(HALF, rest & (HALF - 1)))
+        from_s = jnp.concatenate(
+            [looked_up(send, s[:, i : i + F]) for i in range(0, LOOKED, F)]
+            + [jnp.where((rest & HALF) > 0, by_product[F:], by_product[:F])],
+            axis=1,
+        )
         from_r = dot(recv, hot_r)
         act = silu(
-            jnp.where(up_s, from_s[F:], from_s[:F]) + jnp.where(up_r, from_r[F:], from_r[:F])
+            from_s + jnp.where(up_r, from_r[F:], from_r[:F])
         )
         act = act.astype(bf16)
         spread = jnp.concatenate([jnp.where(up_r, zero, act), jnp.where(up_r, act, zero)], axis=0)
@@ -250,8 +269,12 @@
     upper = columns[:, 1:2]
     stay = columns[:, 2:3]
     both = jnp.concatenate([mesh_out[pl.ds(0, PLANE), :], mesh_out[pl.ds(PLANE, PLANE), :]], axis=1)
-    cells = lax.broadcasted_iota(jnp.int32, (GRP, PLANE), 1)
-    hot = jnp.where(cells == row_at, 1.0, 0.0).astype(bf16)
+    column = jnp.broadcast_to(row_at, (GRP, F)).astype(jnp.int16)
+    lane = lax.broadcasted_iota(jnp.int16, (GRP, F), 1)
+    one, zero = jnp.ones((), bf16), jnp.zeros((), bf16)
+    hot = jnp.concatenate(
+        [jnp.where(lane + jnp.int16(at) == column, one, zero) for at in range(0, PLANE, F)], axis=1
+    )
     found = dot(hot, both)
     near = jnp.where(upper > 0.5, found[:, F:], found[:, :F]).astype(bf16)
     update = dot(edge_sum[...], w_node[:F, :]) + dot(near, w_node[F:, :])

time: 91.9 us -> 91.3 us (level)
  no operation moved by 1% of the time
where the time goes in v6:
time: 91.3 us; the launch traced here: 90.7 us
  Pallas kernels  53.1 us (58%)
  blocking collectives  16.2 us (18%)
  starting transfers between devices  13.1 us (14%)
  waiting for transfers between devices  7.62 us (8%)
    pallas_call x1, Pallas kernels, edges(): pl.pallas_call(edge_kernel, grid=(NGRP,), in_specs=[pl.BlockSpec((GRP, F)...  19.9 us
    pallas_call x1, Pallas kernels, nodes(): pl.pallas_call(node_kernel, grid=(NGRP,), in_specs=[pl.BlockSpec((PLANE,...  19.9 us
    all_to_all x1, blocking collectives, shards(): totals = lax.all_to_all(totals, GX_GY, 0, 0)  16.2 us
    ppermute x8, starting transfers between devices, ring(): lax.ppermute(block, axis, [(i, (i + step) % size) for i in range(size)])  13.1 us
    pallas_call x1, Pallas kernels, encode(): pl.pallas_call(encode_kernel, grid=(NGRP,), in_specs=[pl.BlockSpec((SPAN,...  10 us
    ppermute x8, waiting for transfers between devices, ring(): lax.ppermute(block, axis, [(i, (i + step) % size) for i in range(size)])  7.62 us
  transfers between devices with their start and end apart: 8, of which 2 were waited for; matrix products, arithmetic and copies ran while one was open for 0% of the time, Pallas kernels for 22%

profile of v6, /device:TPU:0, one launch (start us, length us, event | category | flops | bytes accessed | tf_op | source)
XLA Modules:
  0.0 90.7 jit_solution(533192285489917588)
XLA Ops:
  0.6 10.0 %encode.1 = (bf16[16384,128]{1,0:T(8,128)(2,1)}, bf16[16,32,128]{2,1,0:T(8,128)(2,1)}, bf16[16,32,128]{2,1,0:T(8,128)(2,1)}, bf16[1024,128]{1,0:T(8,128)(2,1)}, bf16[1024,128]{1,0:T(8,128)(2,1)}) custom-call(bf16[16384,128]{1,0:T(8,128)(2,1)} %bitcast.6, bf16[4096,128]{1,0:T(8,128)(2,1)} %feat.5, s32[8,1,512]{2,1,0:T(1,128)} %bitcast.10, bf16[128,128]{1,0:T(8,128)(2,1)} %w_enc.1), custom_call_target="tpu_custom_call" | custom-call | tf_op jit(solution)/shard_map/encode/pallas_call | solution.py:92
  10.7 0.1 collective-permute-start
  10.8 6.3 %collective-permute-start.1 = (bf16[1024,128]{1,0:T(8,128)(2,1)}, bf16[1024,128]{1,0:T(8,128)(2,1)S(1)}, u32[]{:S(2)}, u32[]{:S(2)}) collective-permute-start(bf16[1024,128]{1,0:T(8,128)(2,1)} %get-tuple-element.30), channel_id=1, source_target_pairs={{0,120},{8,0},{16,8},{24,16},{32,24},{40,32},{48,40},{56,48},{64,5... | collective-permute-start | bytes 786440 | tf_op jit(solution)/shard_map/ppermute | solution.py:439
  17.0 0.7 collective-permute-start.2
  17.8 3.4 %collective-permute-start.3 = (bf16[16,32,128]{2,1,0:T(8,128)(2,1)}, bf16[16,32,128]{2,1,0:T(8,128)(2,1)S(1)}, u32[]{:S(2)}, u32[]{:S(2)}) collective-permute-start(bf16[16,32,128]{2,1,0:T(8,128)(2,1)} %get-tuple-element.32), channel_id=1, source_target_pairs={{0,7},{1,0},{2,1},{3,2},{4,3},{5,4},{6,5},{7,6},{8,15},{9,8},{10,9... | collective-permute-start | bytes 393224 | tf_op jit(solution)/shard_map/ppermute | solution.py:439
  21.2 19.9 %edges.1 = (bf16[4096,128]{1,0:T(8,128)(2,1)}, s32[8,1,512]{2,1,0:T(1,128)}) custom-call(bf16[4096,128]{1,0:T(8,128)(2,1)} %feat.5, s32[2,24576]{1,0:T(2,128)} %pairs.1, s32[8,1,512]{2,1,0:T(1,128)} %bitcast.7, bf16[128,256]{1,0:T(8,128)(2,1)} %w_pair.1, bf16[128,128]{1,0:T(8,128)(2,1)} %w_edge.1), custom_call_target="tpu_custom_call" | custom-call | tf_op jit(solution)/shard_map/edges/pallas_call | solution.py:173
  41.1 0.0 collective-permute-done.2.y_low
  41.1 0.0 collective-permute-done.3.y_high
  41.1 0.0 collective-permute-done.x_low
  41.1 0.0 collective-permute-done.1.x_high
  41.2 19.9 %nodes.1 = (bf16[16384,128]{1,0:T(8,128)(2,1)}, bf16[4096,128]{1,0:T(8,128)(2,1)}, f32[3,4096]{1,0:T(4,128)}, f32[128,1,4]{2,1,0:T(1,128)}, bf16[432,128]{1,0:T(...) custom-call(bf16[16384,128]{1,0:T(8,128)(2,1)} %get-tuple-element.28.before.here.after, ...), custom_call_target="tpu_custom_call" | custom-call | tf_op jit(solution)/shard_map/nodes/pallas_call | solution.py:323
  61.0 0.2 collective-permute-start.4
  61.2 0.4 collective-permute-start.5
  61.6 2.2 %collective-permute-done.4.from_high = bf16[432,128]{1,0:T(8,128)(2,1)S(1)} collective-permute-done((bf16[432,128]{1,0:T(8,128)(2,1)}, bf16[432,128]{1,0:T(8,128)(2,1)S(1)}, u32[]{:S(2)}, u32[]{:S(2)}) %collective-permute-start.4) | collective-permute-done | bytes 110624 | tf_op jit(solution)/shard_map/ppermute | solution.py:439
  63.9 5.4 %collective-permute-done.5.from_low = bf16[432,128]{1,0:T(8,128)(2,1)S(1)} collective-permute-done((bf16[432,128]{1,0:T(8,128)(2,1)}, bf16[432,128]{1,0:T(8,128)(2,1)S(1)}, u32[]{:S(2)}, u32[]{:S(2)}) %collective-permute-start.5) | collective-permute-done | bytes 110624 | tf_op jit(solution)/shard_map/ppermute | solution.py:439
  69.2 1.5 %relay.1 = (bf16[432,128]{1,0:T(8,128)(2,1)}, bf16[432,128]{1,0:T(8,128)(2,1)}) custom-call(bf16[432,128]{1,0:T(8,128)(2,1)S(1)} %collective-permute-done.4.from_high, bf16[432,128]{1,0:T(8,128)(2,1)S(1)} %collective-permute-done.5.from_low, bf16[144,128]{1,0:T(8,128)(2,1)} %get-tuple-element.39.own_down, bf16[144,128]{1,0:T(8,128)(2,1)} %get-tuple-element.40.own_up), custom_call_target="tpu_custom_call" | custom-call | tf_op jit(solution)/shard_map/relay/pallas_call | solution.py:396
  70.7 0.8 collective-permute-start.6
  71.5 1.2 %collective-permute-start.7 = (bf16[432,128]{1,0:T(8,128)(2,1)}, bf16[432,128]{1,0:T(8,128)(2,1)S(1)}, u32[]{:S(2)}, u32[]{:S(2)}) collective-permute-start(bf16[432,128]{1,0:T(8,128)(2,1)} %get-tuple-element.45), channel_id=1, source_target_pairs={{0,1},{1,2},{2,3},{3,4},{4,5},{5,6},{6,7},{7,0},{8,9},{9,10},{10,1... | collective-permute-start | bytes 331784 | tf_op jit(solution)/shard_map/ppermute | solution.py:439
  72.7 16.2 %all_to_all.5.totals = f32[128,1,4]{2,1,0:T(1,128)} all-to-all(f32[128,1,4]{2,1,0:T(1,128)} %get-tuple-element.46), channel_id=1, replica_groups=mesh['gx_0'=2,'gx_1'=4,'gx_2'=2,'gy_0'=4,'gy_1'=2] {'gx_0','gx_1','gx_2'..., dimensions={0} | all-to-all | bytes 4096 | tf_op jit(solution)/shard_map/all_to_all | solution.py:476
  88.9 0.0 collective-permute-done.6.down
  88.9 0.0 collective-permute-done.7.up
  88.9 1.8 %finish.1 = (bf16[1024,128]{1,0:T(8,128)(2,1)}, f32[4,1024]{1,0:T(4,128)}, f32[3,4096]{1,0:T(4,128)}) custom-call(bf16[432,128]{1,0:T(8,128)(2,1)S(1)} %collective-permute-done.4.from_high, bf16[432,128]{1,0:T(8,128)(2,1)S(1)} %collective-permute-done.5.from_low, bf16[432,128]{1,0:T(8,128)(2,1)S(1)} %collective-permute-done.6.down, ...), custom_call_target="tpu_custom_call" | custom-call | tf_op jit(solution)/shard_map/finish/pallas_call | solution.py:426
Async XLA Ops:
  10.7 30.5 %collective-permute-start = (bf16[1024,128]{1,0:T(8,128)(2,1)}, bf16[1024,128]{1,0:T(8,128)(2,1)S(1)}, u32[]{:S(2)}, u32[]{:S(2)}) collective-permute-start(bf16[1024,128]{1,0:T(8,128)(2,1)} %get-tuple-element.29), channel_id=1, source_target_pairs={{0,8},{8,16},{16,24},{24,32},{32,40},{40,48},{48,56},{56,64},{64,7... | collective-permute-start | bytes 786440 | tf_op jit(solution)/shard_map/ppermute | solution.py:439
  10.8 30.4 %collective-permute-start.1 = (bf16[1024,128]{1,0:T(8,128)(2,1)}, bf16[1024,128]{1,0:T(8,128)(2,1)S(1)}, u32[]{:S(2)}, u32[]{:S(2)}) collective-permute-start(bf16[1024,128]{1,0:T(8,128)(2,1)} %get-tuple-element.30), channel_id=1, source_target_pairs={{0,120},{8,0},{16,8},{24,16},{32,24},{40,32},{48,40},{56,48},{64,5... | collective-permute-start | bytes 786440 | tf_op jit(solution)/shard_map/ppermute | solution.py:439
  17.0 24.1 %collective-permute-start.2 = (bf16[16,32,128]{2,1,0:T(8,128)(2,1)}, bf16[16,32,128]{2,1,0:T(8,128)(2,1)S(1)}, u32[]{:S(2)}, u32[]{:S(2)}) collective-permute-start(bf16[16,32,128]{2,1,0:T(8,128)(2,1)} %get-tuple-element.31), channel_id=1, source_target_pairs={{0,1},{1,2},{2,3},{3,4},{4,5},{5,6},{6,7},{7,0},{8,9},{9,10},{10,1... | collective-permute-start | bytes 393224 | tf_op jit(solution)/shard_map/ppermute | solution.py:439
  17.8 23.3 %collective-permute-start.3 = (bf16[16,32,128]{2,1,0:T(8,128)(2,1)}, bf16[16,32,128]{2,1,0:T(8,128)(2,1)S(1)}, u32[]{:S(2)}, u32[]{:S(2)}) collective-permute-start(bf16[16,32,128]{2,1,0:T(8,128)(2,1)} %get-tuple-element.32), channel_id=1, source_target_pairs={{0,7},{1,0},{2,1},{3,2},{4,3},{5,4},{6,5},{7,6},{8,15},{9,8},{10,9... | collective-permute-start | bytes 393224 | tf_op jit(solution)/shard_map/ppermute | solution.py:439
  61.0 2.8 %collective-permute-start.4 = (bf16[432,128]{1,0:T(8,128)(2,1)}, bf16[432,128]{1,0:T(8,128)(2,1)S(1)}, u32[]{:S(2)}, u32[]{:S(2)}) collective-permute-start(bf16[432,128]{1,0:T(8,128)(2,1)} %get-tuple-element.37), channel_id=1, source_target_pairs={{0,120},{8,0},{16,8},{24,16},{32,24},{40,32},{48,40},{56,48},{64,5... | collective-permute-start | bytes 331784 | tf_op jit(solution)/shard_map/ppermute | solution.py:439
  61.2 8.0 %collective-permute-start.5 = (bf16[432,128]{1,0:T(8,128)(2,1)}, bf16[432,128]{1,0:T(8,128)(2,1)S(1)}, u32[]{:S(2)}, u32[]{:S(2)}) collective-permute-start(bf16[432,128]{1,0:T(8,128)(2,1)} %get-tuple-element.38), channel_id=1, source_target_pairs={{0,8},{8,16},{16,24},{24,32},{32,40},{40,48},{48,56},{56,64},{64,7... | collective-permute-start | bytes 331784 | tf_op jit(solution)/shard_map/ppermute | solution.py:439
  70.7 18.2 %collective-permute-start.6 = (bf16[432,128]{1,0:T(8,128)(2,1)}, bf16[432,128]{1,0:T(8,128)(2,1)S(1)}, u32[]{:S(2)}, u32[]{:S(2)}) collective-permute-start(bf16[432,128]{1,0:T(8,128)(2,1)} %get-tuple-element.44), channel_id=1, source_target_pairs={{0,7},{1,0},{2,1},{3,2},{4,3},{5,4},{6,5},{7,6},{8,15},{9,8},{10,9... | collective-permute-start | bytes 331784 | tf_op jit(solution)/shard_map/ppermute | solution.py:439
  71.5 17.4 %collective-permute-start.7 = (bf16[432,128]{1,0:T(8,128)(2,1)}, bf16[432,128]{1,0:T(8,128)(2,1)S(1)}, u32[]{:S(2)}, u32[]{:S(2)}) collective-permute-start(bf16[432,128]{1,0:T(8,128)(2,1)} %get-tuple-element.45), channel_id=1, source_target_pairs={{0,1},{1,2},{2,3},{3,4},{4,5},{5,6},{6,7},{7,0},{8,9},{9,10},{10,1... | collective-permute-start | bytes 331784 | tf_op jit(solution)/shard_map/ppermute | solution.py:439
